TPU v7x, 256 devices: a whole 4x4x8 slice. The times are simulated.
256 devices in a mesh: section: 4 (over y), dp: 64 (over x, z, core).
Axes of the slice: x: 4, y: 4, z: 8, core: 2. Of those that a mesh axis runs over, the one named last changes fastest.
Arguments:
- grads: float32 [4, 64, 512, 4096], P('section', 'dp'), may hold values from -8192 to 8192
- skipped: int32 [64], P('dp'), may hold values from 0 to 24
- master: float32 [4, 512, 4096], P('section', 'dp'), may hold values from -6 to 6
- moment_one: float32 [4, 512, 4096], P('section', 'dp'), may hold values from -6 to 6
- moment_two: float32 [4, 512, 4096], P('section', 'dp'), may hold values from 0.25 to 4
- bounds: int32 [4, 9], P('section'), may hold values from 0 to 512, as said below
- step: int32 [1], replicated, may hold values from 1 to 24
Outputs:
- params: bfloat16 [4, 512, 4096], P('section')
- master_next: float32 [4, 512, 4096], P('section', 'dp')
- moment_one_next: float32 [4, 512, 4096], P('section', 'dp')
- moment_two_next: float32 [4, 512, 4096], P('section', 'dp')
- layer_norms: float32 [4, 8], P('section')
- grad_norm: float32 [1], replicated
Inputs may be any that keep to these rules, and one draw needn't show every extreme that they name: `bounds`: each section's row is strictly increasing, starts at 0 and ends at 512.
All inputs are finite; a program needn't handle non-finite values.
Results may differ from a plain program's by a relative error of at most 0.001.
Values may be sent and summed in bfloat16 or wider, within the bound.
No kernel may reach another device: no remote copies, remote signals or barrier semaphores. Data moves between devices by JAX's collectives and lax.ppermute only.
A program may use at most 64 MiB of HBM per device.

v0:
```python
import jax
import jax.numpy as jnp
from jax import lax
from jax.sharding import Mesh
from jax.sharding import PartitionSpec as P

MICRO = 32
DP = ("dp_0", "dp_1", "dp_2")


beta_one = 0.9
beta_two = 0.95
learn_rate = 0.05
weight_decay = 0.1
epsilon = 1e-08


def copy_for_each(shard, axis):
    size = lax.axis_size(axis)
    return lax.all_to_all(
        jnp.broadcast_to(shard[None], (size, *shard.shape)), axis, 0, 0, tiled=True
    )


def taken_together(shard, axis):
    everything = copy_for_each(shard, axis)
    return jnp.sum(everything, axis=0)


def joined_along(tiles, dim):
    dims = list(tiles.shape[1:])
    dims[dim] *= tiles.shape[0]
    return jnp.moveaxis(tiles, 0, dim).reshape(dims)


def stacked_from(shard, axes, order):
    tiles = shard
    for k in order:
        tiles = lax.all_gather(tiles, axes[k])
    done = order[::-1]
    back = [done.index(k) for k in range(len(axes))]
    tiles = tiles.transpose(*back, *range(len(axes), tiles.ndim))
    return tiles.reshape(-1, *shard.shape)


def whole_of(shard, axes, order, dim):
    return joined_along(stacked_from(shard, axes, order), dim)


def layer_share(row_squares, bounds, own_rows):
    first_row = lax.axis_index(DP) * own_rows
    row_index = first_row + jnp.arange(own_rows, dtype=jnp.int32)
    inside = (row_index[:, None] >= bounds[0, None, :-1]) & (
        row_index[:, None] < bounds[0, None, 1:]
    )
    return jnp.sum(row_squares[:, None] * inside.astype(jnp.float32), axis=0)


def on_device(grads, skipped, master, moment_one, moment_two, bounds, step):
    flat_grads = grads[0, 0]
    rows_all = flat_grads.shape[0]
    width = flat_grads.shape[1]
    own_rows = master.shape[1]
    n_section = lax.axis_size("section")
    summed = lax.psum_scatter(flat_grads, DP, scatter_dimension=0, tiled=True)
    good_count = (MICRO - skipped[0]).astype(jnp.float32)
    total_good = taken_together(good_count, DP)
    mean_grad = summed / total_good
    layer_part = layer_share(jnp.sum(mean_grad * mean_grad, axis=1), bounds, own_rows)
    layer_sq = taken_together(layer_part, DP)
    total_sq = taken_together(jnp.sum(layer_sq), "section")
    grad_rms = jnp.sqrt(total_sq / (n_section * rows_all * width))
    layer_rows = (bounds[0, 1:] - bounds[0, :-1]).astype(jnp.float32)
    layer_norms = jnp.sqrt(layer_sq / (layer_rows * width))
    clipped = mean_grad / jnp.maximum(1.0, grad_rms)
    first_next = beta_one * moment_one[0] + (1.0 - beta_one) * clipped
    second_next = beta_two * moment_two[0] + (1.0 - beta_two) * clipped * clipped
    step_value = step[0].astype(jnp.float32)
    fix_one = 1.0 - jnp.power(beta_one, step_value)
    fix_two = 1.0 - jnp.power(beta_two, step_value)
    update = first_next / fix_one / (jnp.sqrt(second_next / fix_two) + epsilon)
    master_next = master[0] - learn_rate * (update + weight_decay * master[0])
    gathered = whole_of(master_next.astype(jnp.bfloat16), DP, (0, 1, 2), 0)
    return (
        gathered[None],
        master_next[None],
        first_next[None],
        second_next[None],
        layer_norms[None],
        grad_rms.reshape(1),
    )


def solution(mesh):
    split = Mesh(
        mesh.devices.reshape(mesh.shape["section"], 4, 8, 2), ("section", "dp_0", "dp_1", "dp_2")
    )
    placed = (
        P("section", DP, None, None),
        P(DP),
        P("section", DP, None),
        P("section", DP, None),
        P("section", DP, None),
        P("section", None),
        P(),
    )
    return jax.shard_map(
        on_device,
        mesh=split,
        in_specs=placed,
        out_specs=(
            P("section", None, None),
            P("section", DP, None),
            P("section", DP, None),
            P("section", DP, None),
            P("section", None),
            P(),
        ),
        check_vma=False,
    )
```

profile of v0, /device:TPU:1, one launch (start us, length us, event | category | flops | bytes accessed | tf_op | source)
XLA Modules:
  0.0 281.4 jit_solution(16471129664815366816)
XLA Ops:
  7.3 0.6 reduce-scatter.2.cloned.1.call-update
  8.5 0.6 broadcast_in_dim.12
  9.2 13.0 %all-to-all-start = ((f32[64,1,1]{2,1,0:T(1,128)}), f32[64,1,1]{2,1,0:T(1,128)S(1)}, u32[]{:S(2)}, u32[]{:S(2)}) async-start(f32[64,1,1]{2,1,0:T(1,128)} %broadcast_in_dim.12), calls=%async_computation.1 | async-start | bytes 65536 | tf_op jit(solution)/shard_map/all_to_all | solution.py:20
  22.2 0.1 slice_bitcast_fusion.1
  22.3 9.1 %all-to-all-done = f32[64,1,1]{2,1,0:T(1,128)S(1)} async-done(((f32[64,1,1]{2,1,0:T(1,128)}), f32[64,1,1]{2,1,0:T(1,128)S(1)}, u32[]{:S(2)}, u32[]{:S(2)}) %all-to-all-start) | async-done | bytes 288 | tf_op jit(solution)/shard_map/all_to_all | solution.py:20
  31.4 0.7 reduce_sum.56
  32.1 131.4 %reduce-scatter.2.cloned.1.call-done = f32[8,4096]{1,0:T(8,128)} async-done(((f32[512,4096]{1,0:T(8,128)}), f32[8,4096]{1,0:T(8,128)}) %reduce-scatter.2.cloned.1.call-update) | async-done | bytes 131088 | tf_op jit(solution)/shard_map/reduce_scatter | solution.py:65
  163.5 1.7 multiply_reduce_fusion
  165.2 0.1 select_reduce_fusion
  165.3 0.6 broadcast_in_dim.13
  165.9 12.3 %all-to-all-start.1 = ((f32[64,1,8]{2,1,0:T(1,128)}), f32[64,1,8]{2,1,0:T(1,128)S(1)}, u32[]{:S(2)}, u32[]{:S(2)}) async-start(f32[64,1,8]{2,1,0:T(1,128)} %broadcast_in_dim.13), calls=%async_computation.2 | async-start | bytes 65536 | tf_op jit(solution)/shard_map/all_to_all | solution.py:20
  178.2 0.0 all-gather.6.cloned.1.call-start
  179.0 8.5 %all-to-all-done.1 = f32[64,1,8]{2,1,0:T(1,128)S(1)} async-done(((f32[64,1,8]{2,1,0:T(1,128)}), f32[64,1,8]{2,1,0:T(1,128)S(1)}, u32[]{:S(2)}, u32[]{:S(2)}) %all-to-all-start.1) | async-done | bytes 2080 | tf_op jit(solution)/shard_map/all_to_all | solution.py:20
  187.5 0.7 fusion.6
  188.1 0.6 broadcast_in_dim.14
  188.8 8.0 %all_to_all.18 = f32[4,1,1]{2,1,0:T(1,128)S(1)} all-to-all(f32[4,1,1]{2,1,0:T(1,128)S(1)} %broadcast_in_dim.14), channel_id=1, replica_groups=mesh['section'=4,'dp_0'=4,'dp_1'=8,'dp_2'=2] {'section'}, dimensions={0} | all-to-all | bytes 32 | tf_op jit(solution)/shard_map/all_to_all | solution.py:20
  196.8 0.6 reduce_sum.60
  198.7 1.7 fusion.7
  200.4 10.6 %all-gather = bf16[32,4096]{1,0:T(8,128)(2,1)} all-gather(bf16[8,4096]{1,0:T(8,128)(2,1)S(1)} %get-tuple-element.8), channel_id=2, replica_groups=mesh['section'=4,'dp_0'=4,'dp_1'=8,'dp_2'=2] {'dp_0'}, dimensions={0}, use_global_device_ids=true | all-gather | bytes 327680 | tf_op jit(solution)/shard_map/all_gather | solution.py:39
  211.0 0.0 all-gather.8.cloned.1.call-start
  211.1 33.6 %all-gather.6.cloned.1.call-done = bf16[32,8,4096]{2,1,0:T(8,128)(2,1)} async-done(((bf16[4,8,4096]{2,1,0:T(8,128)(2,1)}), bf16[32,8,4096]{2,1,0:T(8,128)(2,1)}) %all-gather.6.cloned.1.call-update) | async-done | bytes 2097168 | tf_op jit(solution)/shard_map/all_gather | solution.py:39
  244.7 0.6 fusion.3
  245.3 23.7 %all-gather.8.cloned.1.call-done = bf16[16,4,8,4096]{3,2,1,0:T(8,128)(2,1)} async-done(((bf16[8,4,8,4096]{3,2,1,0:T(8,128)(2,1)}), bf16[16,4,8,4096]{3,2,1,0:T(8,128)(2,1)}) %all-gather.8.cloned.1.call-update) | async-done | bytes 4194320 | tf_op jit(solution)/shard_map/all_gather | solution.py:39
  269.0 4.7 %copy.19 = bf16[4,8,2,8,4096]{4,3,2,1,0:T(8,128)(2,1)} copy(bf16[4,8,2,8,4096]{4,3,0,1,2:T(8,128)(2,1)} %bitcast.50) | data formatting | bytes 8388608 | tf_op jit(solution)/shard_map/transpose | solution.py:42
  (12 shorter events, 0.1 us)
Async XLA Ops:
  7.2 156.3 %reduce-scatter.2.cloned.1.call-start = ((), (), s32[]{:S(2)}) async-start(), calls=%async_computation.4 | async-start | bytes 8519680 | tf_op jit(solution)/shard_map/reduce_scatter | solution.py:65
  7.2 15.0 %copy-start.3 = (s32[1,9]{1,0:T(1,128)S(1)}, s32[1,9]{1,0:T(1,128)}, u32[]{:S(2)}) copy-start(s32[1,9]{1,0:T(1,128)} %param.12) | copy-start | bytes 112
  7.2 191.5 %copy-start = (f32[1,8,4096]{2,1,0:T(8,128)S(1)}, f32[1,8,4096]{2,1,0:T(8,128)}, u32[]{:S(2)}) copy-start(f32[1,8,4096]{2,1,0:T(8,128)} %param.11) | copy-start | bytes 393220
  7.2 191.5 %copy-start.1 = (f32[1,8,4096]{2,1,0:T(8,128)S(1)}, f32[1,8,4096]{2,1,0:T(8,128)}, u32[]{:S(2)}) copy-start(f32[1,8,4096]{2,1,0:T(8,128)} %param.10) | copy-start | bytes 393220
  7.2 191.5 %copy-start.2 = (f32[1,8,4096]{2,1,0:T(8,128)S(1)}, f32[1,8,4096]{2,1,0:T(8,128)}, u32[]{:S(2)}) copy-start(f32[1,8,4096]{2,1,0:T(8,128)} %param.9) | copy-start | bytes 393220
  9.2 22.2 %all-to-all-start = ((f32[64,1,1]{2,1,0:T(1,128)}), f32[64,1,1]{2,1,0:T(1,128)S(1)}, u32[]{:S(2)}, u32[]{:S(2)}) async-start(f32[64,1,1]{2,1,0:T(1,128)} %broadcast_in_dim.12), calls=%async_computation.1 | async-start | bytes 65536 | tf_op jit(solution)/shard_map/all_to_all | solution.py:20
  165.9 21.5 %all-to-all-start.1 = ((f32[64,1,8]{2,1,0:T(1,128)}), f32[64,1,8]{2,1,0:T(1,128)S(1)}, u32[]{:S(2)}, u32[]{:S(2)}) async-start(f32[64,1,8]{2,1,0:T(1,128)} %broadcast_in_dim.13), calls=%async_computation.2 | async-start | bytes 65536 | tf_op jit(solution)/shard_map/all_to_all | solution.py:20
  178.2 66.5 %all-gather.6.cloned.1.call-start = ((), (), s32[]{:S(2)}) async-start(), calls=%async_computation.5 | async-start | bytes 2359296 | tf_op jit(solution)/shard_map/all_gather | solution.py:39
  211.0 58.0 %all-gather.8.cloned.1.call-start = ((), (), s32[]{:S(2)}) async-start(), calls=%async_computation.6 | async-start | bytes 6291456 | tf_op jit(solution)/shard_map/all_gather | solution.py:39
Sparse Core Ops, SparseCore 0:
  12.2 151.2 reduce-scatter.1
  211.1 33.5 all-gather.5
  246.5 22.4 all-gather.7
where the time goes:
time: 282 us; the launch traced here: 281 us
  waiting for transfers between devices  207 us (73%)
  starting transfers between devices  25.4 us (9%)
  blocking collectives  18.5 us (7%)
  between operations  17.7 us (6%)
  local copies, waits for them, and re-layouts  6.71 us (2%)
  other arithmetic  6.04 us (2%)
    reduce_scatter x1, waiting for transfers between devices, on_device(): summed = lax.psum_scatter(flat_grads, DP, scatter_dimension=0, tiled=True)  131 us
    all_gather x2, waiting for transfers between devices, stacked_from(): tiles = lax.all_gather(tiles, axes[k])  57.3 us
    all_to_all x2, starting transfers between devices, copy_for_each(): lax.all_to_all(jnp.broadcast_to(shard[None], (size, *shard.shape)), axis,...  25.3 us
    all_to_all x2, waiting for transfers between devices, copy_for_each(): lax.all_to_all(jnp.broadcast_to(shard[None], (size, *shard.shape)), axis,...  17.6 us
    all_gather x1, blocking collectives, stacked_from(): tiles = lax.all_gather(tiles, axes[k])  10.6 us
    all_to_all x1, blocking collectives, copy_for_each(): lax.all_to_all(jnp.broadcast_to(shard[None], (size, *shard.shape)), axis,...  7.95 us
  transfers between devices with their start and end apart: 5, of which 5 were waited for; matrix products, arithmetic and copies ran while one was open for 1% of the time, Pallas kernels for 0%

commit v1 on v0

v1 whole, which is shorter than its diff:
```python
import jax
import jax.numpy as jnp
from jax import lax
from jax.sharding import Mesh
from jax.sharding import PartitionSpec as P

MICRO = 32
DP = ("x", "z", "c")
ALL = ("section", "x", "z", "c")

beta_one = 0.9
beta_two = 0.95
learn_rate = 0.05
weight_decay = 0.1
epsilon = 1e-08

WIRE = jnp.float16
SCALE = 0.5


def swapped(value):
    return lax.ppermute(value, "c", [(0, 1), (1, 0)])


def exchanged(value, axis):
    return lax.all_to_all(value, axis, 0, 0, tiled=True)


def reduced_rows(flat, own_rows):
    n_x, n_z, n_c = (lax.axis_size(a) for a in DP)
    core = lax.axis_index("c")
    parts = flat.reshape(n_x, n_z, n_c, own_rows, flat.shape[1])
    kept = lax.dynamic_index_in_dim(parts, core, 2, keepdims=False) * SCALE
    sent = lax.dynamic_index_in_dim(parts, 1 - core, 2, keepdims=False) * SCALE
    chip = kept + swapped(sent.astype(WIRE)).astype(jnp.float32)
    along_x = exchanged(chip.astype(WIRE), "x").astype(jnp.float32).sum(axis=0)
    along_z = exchanged(along_x.astype(WIRE), "z").astype(jnp.float32).sum(axis=0)
    return along_z * (1.0 / SCALE)


def gathered_rows(rows):
    n_x, n_z, n_c = (lax.axis_size(a) for a in DP)
    core = lax.axis_index("c")
    along_z = exchanged(jnp.broadcast_to(rows[None], (n_z, *rows.shape)), "z")
    along_x = exchanged(jnp.broadcast_to(along_z[None], (n_x, *along_z.shape)), "x")
    other = swapped(along_x)
    first = core == 0
    both = jnp.stack(
        [jnp.where(first, along_x, other), jnp.where(first, other, along_x)], axis=2
    )
    return both.reshape(n_x * n_z * n_c * rows.shape[0], rows.shape[1])


def on_device(grads, skipped, master, moment_one, moment_two, bounds, step):
    flat_grads = grads[0, 0]
    rows_all, width = flat_grads.shape
    own_rows = master.shape[1]
    layers = bounds.shape[1] - 1
    n_section = lax.axis_size("section")
    n_all = lax.axis_size(ALL)
    summed = reduced_rows(flat_grads, own_rows)

    row_index = lax.axis_index(DP) * own_rows + jnp.arange(own_rows, dtype=jnp.int32)
    inside = (row_index[:, None] >= bounds[0, None, :-1]) & (
        row_index[:, None] < bounds[0, None, 1:]
    )
    row_squares = jnp.sum(summed * summed, axis=1)
    layer_part = jnp.sum(row_squares[:, None] * inside.astype(jnp.float32), axis=0)
    good = (MICRO - skipped).astype(jnp.float32)
    report = jnp.concatenate([layer_part, good])
    reports = exchanged(jnp.broadcast_to(report[None], (n_all, layers + 1)), ALL)
    sections = reports.reshape(n_section, -1, layers + 1).sum(axis=1)
    total_good = sections[0, layers]
    squares = sections[:, :layers] / (total_good * total_good)
    layer_sq = lax.dynamic_index_in_dim(
        squares, lax.axis_index("section"), 0, keepdims=False
    )
    grad_rms = jnp.sqrt(jnp.sum(squares) / (n_section * rows_all * width))
    layer_rows = (bounds[0, 1:] - bounds[0, :-1]).astype(jnp.float32)
    layer_norms = jnp.sqrt(layer_sq / (layer_rows * width))

    clipped = summed / total_good / jnp.maximum(1.0, grad_rms)
    first_next = beta_one * moment_one[0] + (1.0 - beta_one) * clipped
    second_next = beta_two * moment_two[0] + (1.0 - beta_two) * clipped * clipped
    step_value = step[0].astype(jnp.float32)
    fix_one = 1.0 - jnp.power(beta_one, step_value)
    fix_two = 1.0 - jnp.power(beta_two, step_value)
    update = first_next / fix_one / (jnp.sqrt(second_next / fix_two) + epsilon)
    master_next = master[0] - learn_rate * (update + weight_decay * master[0])
    gathered = gathered_rows(master_next.astype(jnp.bfloat16))
    return (
        gathered[None],
        master_next[None],
        first_next[None],
        second_next[None],
        layer_norms[None],
        grad_rms.reshape(1),
    )


def solution(mesh):
    split = Mesh(
        mesh.devices.reshape(mesh.shape["section"], 4, 8, 2), ("section", "x", "z", "c")
    )
    placed = (
        P("section", DP, None, None),
        P(DP),
        P("section", DP, None),
        P("section", DP, None),
        P("section", DP, None),
        P("section", None),
        P(),
    )
    return jax.shard_map(
        on_device,
        mesh=split,
        in_specs=placed,
        out_specs=(
            P("section", None, None),
            P("section", DP, None),
            P("section", DP, None),
            P("section", DP, None),
            P("section", None),
            P(),
        ),
        check_vma=False,
    )
```

time: 282 us -> 152 us (0.54)
  waiting for transfers between devices: 207 us -> 34.1 us
  blocking collectives: 18.5 us -> 73.6 us
  between operations: 17.7 us -> 5.92 us
  other arithmetic: 6.04 us -> 13.5 us
  local copies, waits for them, and re-layouts: 6.71 us -> 2.53 us
  starting transfers between devices: 25.4 us -> 22.3 us
    reduce_scatter x1 -> x0, waiting for transfers between devices: 131 us -> none  [on_device(): summed = lax.psum_scatter(flat_grads, DP, scatter_dimension=0, tiled=True)]
    all_to_all x1 -> x3, blocking collectives: 7.95 us -> 73.6 us  [exchanged(): return lax.all_to_all(value, axis, 0, 0, tiled=True)]
    all_gather x2 -> x0, waiting for transfers between devices: 57.3 us -> none  [stacked_from(): tiles = lax.all_gather(tiles, axes[k])]
    all_gather x1 -> x0, blocking collectives: 10.6 us -> none  [stacked_from(): tiles = lax.all_gather(tiles, axes[k])]
    all_to_all x2, starting transfers between devices: 25.3 us -> 15.6 us  [exchanged(): return lax.all_to_all(value, axis, 0, 0, tiled=True)]
    all_to_all x2, waiting for transfers between devices: 17.6 us -> 27.1 us  [exchanged(): return lax.all_to_all(value, axis, 0, 0, tiled=True)]
    ppermute x0 -> x2, waiting for transfers between devices: none -> 7 us  [swapped(): return lax.ppermute(value, 'c', [(0, 1), (1, 0)])]
    ppermute x0 -> x2, starting transfers between devices: none -> 6.64 us  [swapped(): return lax.ppermute(value, 'c', [(0, 1), (1, 0)])]
  transfers between devices with their start and end apart: 5 -> 4, of which waited for: 5 -> 4; matrix products, arithmetic and copies ran while one was open for 1% -> 1% of each run, Pallas kernels for 0% -> 0%
where the time goes in v1:
time: 152 us
  blocking collectives  73.6 us (48%)
  waiting for transfers between devices  34.1 us (22%)
  starting transfers between devices  22.3 us (15%)
  other arithmetic  13.5 us (9%)
  between operations  5.92 us (4%)
  local copies, waits for them, and re-layouts  2.53 us (2%)
    all_to_all x3, blocking collectives, exchanged(): return lax.all_to_all(value, axis, 0, 0, tiled=True)  73.6 us
    all_to_all x2, waiting for transfers between devices, exchanged(): return lax.all_to_all(value, axis, 0, 0, tiled=True)  27.1 us
    all_to_all x2, starting transfers between devices, exchanged(): return lax.all_to_all(value, axis, 0, 0, tiled=True)  15.6 us
    ppermute x2, waiting for transfers between devices, swapped(): return lax.ppermute(value, 'c', [(0, 1), (1, 0)])  7 us
    ppermute x2, starting transfers between devices, swapped(): return lax.ppermute(value, 'c', [(0, 1), (1, 0)])  6.64 us
    another operation x2, other arithmetic, gathered_rows(): jnp.stack([jnp.where(first, along_x, other), jnp.where(first, other, alon...  4.24 us
    convert_element_type x1, other arithmetic, reduced_rows(): along_x = exchanged(chip.astype(WIRE), 'x').astype(jnp.float32).sum(axis=0)  3.5 us
  transfers between devices with their start and end apart: 4, of which 4 were waited for; matrix products, arithmetic and copies ran while one was open for 1% of the time, Pallas kernels for 0%

profile of v1, /device:TPU:1, one launch (start us, length us, event | category | flops | bytes accessed | tf_op | source)
XLA Modules:
  0.0 151.9 jit_solution(16201823846856924430)
XLA Ops:
  0.6 2.6 %fusion.4 = f16[4,8,8,4096]{3,2,1,0:T(8,128)(2,1)S(1)} fusion(f32[4,8,2,8,4096]{4,3,2,1,0:T(8,128)} %bitcast.53, s32[]{:T(128)S(6)} %select_n.25), kind=kLoop, calls=%fused_computation.8 | loop fusion | flops 2097152 | bytes 6291460 | tf_op jit(solution)/shard_map/convert_element_type | solution.py:35
  3.2 3.3 %collective-permute-start = (f16[4,8,8,4096]{3,2,1,0:T(8,128)(2,1)S(1)}, f16[4,8,8,4096]{3,2,1,0:T(8,128)(2,1)}, u32[]{:S(2)}, u32[]{:S(2)}) collective-permute-start(f16[4,8,8,4096]{3,2,1,0:T(8,128)(2,1)S(1)} %fusion.4), channel_id=1, source_target_pairs={{0,1},{1,0},{2,3},{3,2},{4,5},{5,4},{6,7},{7,6},{8,9},{9,8},{10,11... | collective-permute-start | bytes 6291464 | tf_op jit(solution)/shard_map/ppermute | solution.py:22
  6.5 3.9 %collective-permute-done = f16[4,8,8,4096]{3,2,1,0:T(8,128)(2,1)} collective-permute-done((f16[4,8,8,4096]{3,2,1,0:T(8,128)(2,1)S(1)}, f16[4,8,8,4096]{3,2,1,0:T(8,128)(2,1)}, u32[]{:S(2)}, u32[]{:S(2)}) %collective-permute-start) | collective-permute-done | bytes 2097184 | tf_op jit(solution)/shard_map/ppermute | solution.py:22
  10.4 3.5 %fusion.2 = f16[4,8,8,4096]{3,2,1,0:T(8,128)(2,1)S(1)} fusion(f16[4,8,8,4096]{3,2,1,0:T(8,128)(2,1)} %collective-permute-done, f32[4,8,2,8,4096]{4,3,2,1,0:T(8,128)} %bitcast.54, s32[]{:T(128)S(6)} %select_n.24), kind=kLoop, calls=%fused_computation.4 | loop fusion | flops 4194304 | bytes 8388612 | tf_op jit(solution)/shard_map/convert_element_type | solution.py:36
  13.9 28.5 %all_to_all.26 = f16[4,8,8,4096]{3,2,1,0:T(8,128)(2,1)S(1)} all-to-all(f16[4,8,8,4096]{3,2,1,0:T(8,128)(2,1)S(1)} %fusion.2), channel_id=1, replica_groups=mesh['section'=4,'x'=4,'z'=8,'c'=2] {'x'}, dimensions={0} | all-to-all | bytes 4194304 | tf_op jit(solution)/shard_map/all_to_all | solution.py:26
  42.5 0.4 convert_reduce_fusion
  42.9 0.8 convert_element_type.42
  43.8 7.2 %all-to-all-start.1 = ((f16[8,8,4096]{2,1,0:T(8,128)(2,1)}), f16[8,8,4096]{2,1,0:T(8,128)(2,1)S(1)}, u32[]{:S(2)}, u32[]{:S(2)}) async-start(f16[8,8,4096]{2,1,0:T(8,128)(2,1)} %convert_element_type.42), calls=%async_computation.1 | async-start | bytes 1048576 | tf_op jit(solution)/shard_map/all_to_all | solution.py:26
  51.8 15.0 %all-to-all-done.1 = f16[8,8,4096]{2,1,0:T(8,128)(2,1)S(1)} async-done(((f16[8,8,4096]{2,1,0:T(8,128)(2,1)}), f16[8,8,4096]{2,1,0:T(8,128)(2,1)S(1)}, u32[]{:S(2)}, u32[]{:S(2)}) %all-to-all-start.1) | async-done | bytes 524320 | tf_op jit(solution)/shard_map/all_to_all | solution.py:26
  66.8 0.1 multiply_reduce_fusion
  67.2 0.7 broadcast_in_dim.8
  67.9 8.4 %all-to-all-start.2 = ((f32[256,1,9]{2,1,0:T(1,128)}), f32[256,1,9]{2,1,0:T(1,128)S(1)}, u32[]{:S(2)}, u32[]{:S(2)}) async-start(f32[256,1,9]{2,1,0:T(1,128)} %broadcast_in_dim.8), calls=%async_computation.2 | async-start | bytes 262144 | tf_op jit(solution)/shard_map/all_to_all | solution.py:26
  77.0 12.1 %all-to-all-done.2 = f32[256,1,9]{2,1,0:T(1,128)S(1)} async-done(((f32[256,1,9]{2,1,0:T(1,128)}), f32[256,1,9]{2,1,0:T(1,128)S(1)}, u32[]{:S(2)}, u32[]{:S(2)}) %all-to-all-start.2) | async-done | bytes 9248 | tf_op jit(solution)/shard_map/all_to_all | solution.py:26
  89.1 0.6 slice.16
  91.1 0.6 fusion.9
  93.1 0.8 convert_bitcast_fusion
  93.9 18.7 %all_to_all.27 = bf16[8,8,4096]{2,1,0:T(8,128)(2,1)S(1)} all-to-all(bf16[8,8,4096]{2,1,0:T(8,128)(2,1)S(1)} %broadcast_in_dim.10), channel_id=1, replica_groups=mesh['section'=4,'x'=4,'z'=8,'c'=2] {'z'}, dimensions={0} | all-to-all | bytes 1048576 | tf_op jit(solution)/shard_map/all_to_all | solution.py:26
  112.6 0.2 broadcast_in_dim.11
  112.8 26.4 %all_to_all.28 = bf16[4,8,8,4096]{3,2,1,0:T(8,128)(2,1)S(1)} all-to-all(bf16[4,8,8,4096]{3,2,1,0:T(8,128)(2,1)S(1)} %broadcast_in_dim.11), channel_id=1, replica_groups=mesh['section'=4,'x'=4,'z'=8,'c'=2] {'x'}, dimensions={0} | all-to-all | bytes 4194304 | tf_op jit(solution)/shard_map/all_to_all | solution.py:26
  139.2 3.4 %collective-permute-start.1 = (bf16[4,8,8,4096]{3,2,1,0:T(8,128)(2,1)S(1)}, bf16[4,8,8,4096]{3,2,1,0:T(8,128)(2,1)}, u32[]{:S(2)}, u32[]{:S(2)}) collective-permute-start(bf16[4,8,8,4096]{3,2,1,0:T(8,128)(2,1)S(1)} %all_to_all.28), channel_id=1, source_target_pairs={{0,1},{1,0},{2,3},{3,2},{4,5},{5,4},{6,7},{7,6},{8,9},{9,8},{10,11... | collective-permute-start | bytes 6291464 | tf_op jit(solution)/shard_map/ppermute | solution.py:22
  142.8 0.6 copy.34
  143.4 3.1 %collective-permute-done.1 = bf16[4,8,8,4096]{3,2,1,0:T(8,128)(2,1)} collective-permute-done((bf16[4,8,8,4096]{3,2,1,0:T(8,128)(2,1)S(1)}, bf16[4,8,8,4096]{3,2,1,0:T(8,128)(2,1)}, u32[]{:S(2)}, u32[]{:S(2)}) %collective-permute-start.1) | collective-permute-done | bytes 2097184 | tf_op jit(solution)/shard_map/ppermute | solution.py:22
  146.5 1.9 %select_bitcast_fusion.1 = (bf16[4,8,1,8,4096]{4,3,2,1,0:T(8,128)(2,1)S(1)}, bf16[4,8,1,8,4096]{4,3,2,1,0:T(8,128)(2,1)S(1)}) fusion(bf16[4,8,8,4096]{3,2,1,0:T(8,128)(2,1)S(1)} %all_to_all.28, bf16[4,8,8,4096]{3,2,1,0:T(8,128)(2,1)} %collective-permute-done.1, pred[]{:T(512)S(6)} %eq.3), kind=kLoop, calls=%fused_computation.10 | loop fusion | flops 2097152 | bytes 8388609 | tf_op jit(solution)/shard_map/stack | solution.py:48
  148.4 2.4 %pad_maximum_fusion = bf16[4,8,2,8,4096]{4,3,2,1,0:T(8,128)(2,1)} fusion(bf16[4,8,1,8,4096]{4,3,2,1,0:T(8,128)(2,1)S(1)} %get-tuple-element.31, bf16[4,8,1,8,4096]{4,3,2,1,0:T(8,128)(2,1)S(1)} %get-tuple-element.30), kind=kLoop, calls=%fused_computation | loop fusion | flops 2097152 | bytes 8388608 | tf_op jit(solution)/shard_map/stack | solution.py:48
  (19 shorter events, 0.7 us)
Async XLA Ops:
  3.2 7.2 %collective-permute-start = (f16[4,8,8,4096]{3,2,1,0:T(8,128)(2,1)S(1)}, f16[4,8,8,4096]{3,2,1,0:T(8,128)(2,1)}, u32[]{:S(2)}, u32[]{:S(2)}) collective-permute-start(f16[4,8,8,4096]{3,2,1,0:T(8,128)(2,1)S(1)} %fusion.4), channel_id=1, source_target_pairs={{0,1},{1,0},{2,3},{3,2},{4,5},{5,4},{6,7},{7,6},{8,9},{9,8},{10,11... | collective-permute-start | bytes 6291464 | tf_op jit(solution)/shard_map/ppermute | solution.py:22
  42.9 8.8 %copy-start.3 = (s32[1,9]{1,0:T(1,128)S(1)}, s32[1,9]{1,0:T(1,128)}, u32[]{:S(2)}) copy-start(s32[1,9]{1,0:T(1,128)} %param.12) | copy-start | bytes 112
  42.9 50.1 %copy-start = (f32[1,8,4096]{2,1,0:T(8,128)S(1)}, f32[1,8,4096]{2,1,0:T(8,128)}, u32[]{:S(2)}) copy-start(f32[1,8,4096]{2,1,0:T(8,128)} %param.9) | copy-start | bytes 393220
  42.9 50.1 %copy-start.1 = (f32[1,8,4096]{2,1,0:T(8,128)S(1)}, f32[1,8,4096]{2,1,0:T(8,128)}, u32[]{:S(2)}) copy-start(f32[1,8,4096]{2,1,0:T(8,128)} %param.11) | copy-start | bytes 393220
  42.9 50.1 %copy-start.2 = (f32[1,8,4096]{2,1,0:T(8,128)S(1)}, f32[1,8,4096]{2,1,0:T(8,128)}, u32[]{:S(2)}) copy-start(f32[1,8,4096]{2,1,0:T(8,128)} %param.10) | copy-start | bytes 393220
  43.8 23.0 %all-to-all-start.1 = ((f16[8,8,4096]{2,1,0:T(8,128)(2,1)}), f16[8,8,4096]{2,1,0:T(8,128)(2,1)S(1)}, u32[]{:S(2)}, u32[]{:S(2)}) async-start(f16[8,8,4096]{2,1,0:T(8,128)(2,1)} %convert_element_type.42), calls=%async_computation.1 | async-start | bytes 1048576 | tf_op jit(solution)/shard_map/all_to_all | solution.py:26
  67.9 21.2 %all-to-all-start.2 = ((f32[256,1,9]{2,1,0:T(1,128)}), f32[256,1,9]{2,1,0:T(1,128)S(1)}, u32[]{:S(2)}, u32[]{:S(2)}) async-start(f32[256,1,9]{2,1,0:T(1,128)} %broadcast_in_dim.8), calls=%async_computation.2 | async-start | bytes 262144 | tf_op jit(solution)/shard_map/all_to_all | solution.py:26
  139.2 7.3 %collective-permute-start.1 = (bf16[4,8,8,4096]{3,2,1,0:T(8,128)(2,1)S(1)}, bf16[4,8,8,4096]{3,2,1,0:T(8,128)(2,1)}, u32[]{:S(2)}, u32[]{:S(2)}) collective-permute-start(bf16[4,8,8,4096]{3,2,1,0:T(8,128)(2,1)S(1)} %all_to_all.28), channel_id=1, source_target_pairs={{0,1},{1,0},{2,3},{3,2},{4,5},{5,4},{6,7},{7,6},{8,9},{9,8},{10,11... | collective-permute-start | bytes 6291464 | tf_op jit(solution)/shard_map/ppermute | solution.py:22

commit v2 on v1

--- a/solution.py
+++ b/solution.py
@@ -1,8 +1,11 @@
 import jax
 import jax.numpy as jnp
 from jax import lax
+from jax.experimental import pallas as pl
+from jax.experimental.pallas import tpu as pltpu
 from jax.sharding import Mesh
 from jax.sharding import PartitionSpec as P
+
 
 MICRO = 32
 DP = ("x", "z", "c")
@@ -17,38 +20,122 @@
 WIRE = jnp.float16
 SCALE = 0.5
 
+SUM_SHARE = 7
+GATHER_SHARE = 6
+
 
 def swapped(value):
     return lax.ppermute(value, "c", [(0, 1), (1, 0)])
 
 
+def shifted(value, axis, k):
+    n = lax.axis_size(axis)
+    return lax.ppermute(value, axis, [(i, (i + k) % n) for i in range(n)])
+
+
 def exchanged(value, axis):
     return lax.all_to_all(value, axis, 0, 0, tiled=True)
 
 
+def hops(n):
+    return sorted(range(1, n), key=lambda k: -min(k, n - k))
+
+
+def piece(parts, at_x, core, first, width):
+    n_x, n_z, _, rows, _ = parts.shape
+    start = (0 if at_x is None else at_x, 0, core, 0, first)
+    taken = (n_x if at_x is None else 1, n_z, 1, rows, width)
+    return lax.dynamic_slice(parts, start, taken)[:, :, 0] * SCALE
+
+
+def at(values, i):
+    return lax.dynamic_index_in_dim(values, i, 0, keepdims=False).astype(jnp.float32)
+
+
 def reduced_rows(flat, own_rows):
     n_x, n_z, n_c = (lax.axis_size(a) for a in DP)
-    core = lax.axis_index("c")
-    parts = flat.reshape(n_x, n_z, n_c, own_rows, flat.shape[1])
-    kept = lax.dynamic_index_in_dim(parts, core, 2, keepdims=False) * SCALE
-    sent = lax.dynamic_index_in_dim(parts, 1 - core, 2, keepdims=False) * SCALE
-    chip = kept + swapped(sent.astype(WIRE)).astype(jnp.float32)
-    along_x = exchanged(chip.astype(WIRE), "x").astype(jnp.float32).sum(axis=0)
-    along_z = exchanged(along_x.astype(WIRE), "z").astype(jnp.float32).sum(axis=0)
-    return along_z * (1.0 / SCALE)
+    x, core = lax.axis_index("x"), lax.axis_index("c")
+    width = flat.shape[1]
+    parts = flat.reshape(n_x, n_z, n_c, own_rows, width)
+    wide = width * SUM_SHARE // 8
+
+    def chip_a(k):
+        to_x = (x + k) % n_x
+        sent = piece(parts, to_x, 1 - core, 0, wide)[0].astype(WIRE)
+        return piece(parts, to_x, core, 0, wide)[0] + swapped(sent).astype(jnp.float32)
+
+    arrived = [shifted(chip_a(k).astype(WIRE), "x", k) for k in hops(n_x)]
+    a_x = chip_a(0)
+    sent = piece(parts, None, 1 - core, wide, width - wide).astype(WIRE)
+    chip_b = piece(parts, None, core, wide, width - wide)
+    chip_b = chip_b + swapped(sent).astype(jnp.float32)
+    b_z = exchanged(chip_b.astype(WIRE).transpose(1, 0, 2, 3), "z")
+    b_z = b_z.astype(jnp.float32).sum(axis=0)
+    for value in arrived:
+        a_x = a_x + value.astype(jnp.float32)
+    b_sent = [shifted(at(b_z, (x + k) % n_x).astype(WIRE), "x", k) for k in hops(n_x)]
+    a_z = exchanged(a_x.astype(WIRE), "z").astype(jnp.float32).sum(axis=0)
+    b_x = at(b_z, x)
+    for value in b_sent:
+        b_x = b_x + value.astype(jnp.float32)
+    return jnp.concatenate([a_z, b_x], axis=1) * (1.0 / SCALE)
+
+
+def placed_rows(slots, a_parts, b_part, out=None):
+    n_x = len(a_parts)
+    n_z, rows, wide = a_parts[0].shape
+    narrow = b_part.shape[-1]
+
+    def kernel(*refs):
+        slots, a_in, b_in = refs[0], refs[1 : 1 + n_x], refs[1 + n_x]
+        to, sems = refs[-2:]
+        copies = []
+        for j in range(n_x):
+            there = to.at[slots[1 + j], :, slots[0]]
+            copies.append((a_in[j], there.at[:, :, pl.ds(0, wide)]))
+            copies.append((b_in.at[:, j], there.at[:, :, pl.ds(wide, narrow)]))
+        copies = [
+            pltpu.make_async_copy(*pair, sems.at[i]) for i, pair in enumerate(copies)
+        ]
+        for copy in copies:
+            copy.start()
+        for copy in copies:
+            copy.wait()
+
+    near = pl.BlockSpec(memory_space=pltpu.VMEM)
+    far = pl.BlockSpec(memory_space=pltpu.HBM)
+    operands = [slots, *a_parts, b_part] + ([] if out is None else [out])
+    specs = [pl.BlockSpec(memory_space=pltpu.SMEM)] + [near] * (n_x + 1)
+    return pl.pallas_call(
+        kernel,
+        out_shape=jax.ShapeDtypeStruct(
+            (n_x, n_z, 2, rows, wide + narrow), a_parts[0].dtype
+        ),
+        in_specs=specs + [far] * (len(operands) - len(specs)),
+        out_specs=far,
+        scratch_shapes=[pltpu.SemaphoreType.DMA((2 * n_x,))],
+        input_output_aliases={} if out is None else {len(operands) - 1: 0},
+        compiler_params=pltpu.CompilerParams(vmem_limit_bytes=8 << 20),
+    )(*operands)
 
 
 def gathered_rows(rows):
     n_x, n_z, n_c = (lax.axis_size(a) for a in DP)
-    core = lax.axis_index("c")
-    along_z = exchanged(jnp.broadcast_to(rows[None], (n_z, *rows.shape)), "z")
-    along_x = exchanged(jnp.broadcast_to(along_z[None], (n_x, *along_z.shape)), "x")
-    other = swapped(along_x)
-    first = core == 0
-    both = jnp.stack(
-        [jnp.where(first, along_x, other), jnp.where(first, other, along_x)], axis=2
-    )
-    return both.reshape(n_x * n_z * n_c * rows.shape[0], rows.shape[1])
+    x, core = lax.axis_index("x"), lax.axis_index("c")
+    own_rows, width = rows.shape
+    wide = width * GATHER_SHARE // 8
+    shifts = [0] + hops(n_x)
+    a, b = rows[:, :wide], rows[:, wide:]
+    b_x = jnp.stack([b] + [shifted(b, "x", k) for k in shifts[1:]])
+    a_z = exchanged(jnp.broadcast_to(a[None], (n_z, *a.shape)), "z")
+    a_all = [a_z] + [shifted(a_z, "x", k) for k in shifts[1:]]
+    b_all = exchanged(jnp.broadcast_to(b_x[None], (n_z, *b_x.shape)), "z")
+    a_other = [swapped(v) for v in a_all]
+    b_other = swapped(b_all)
+    origins = [lax.rem(x + (n_x - k), n_x) for k in shifts]
+    out = placed_rows(jnp.stack([core] + origins), a_all, b_all)
+    out = placed_rows(jnp.stack([1 - core] + origins), a_other, b_other, out)
+    return out.reshape(n_x * n_z * n_c * own_rows, width)
 
 
 def on_device(grads, skipped, master, moment_one, moment_two, bounds, step):
@@ -111,6 +198,7 @@
         P("section", None),
         P(),
     )
+
     return jax.shard_map(
         on_device,
         mesh=split,

time: 152 us -> 141 us (0.928)
  blocking collectives: 73.6 us -> 0 us
  starting transfers between devices: 22.3 us -> 51.9 us
  waiting for transfers between devices: 34.1 us -> 58.5 us
  Pallas kernels: 0 us -> 4.42 us
  local copies, waits for them, and re-layouts: 2.53 us -> 5.4 us
    all_to_all x3 -> x0, blocking collectives: 73.6 us -> none  [exchanged(): return lax.all_to_all(value, axis, 0, 0, tiled=True)]
    ppermute x0 -> x12, waiting for transfers between devices: none -> 16.6 us  [shifted(): return lax.ppermute(value, axis, [(i, (i + k) % n) for i in range(n)])]
    all_to_all x2 -> x5, waiting for transfers between devices: 27.1 us -> 41.9 us  [exchanged(): return lax.all_to_all(value, axis, 0, 0, tiled=True)]
    ppermute x0 -> x12, starting transfers between devices: none -> 14.6 us  [shifted(): return lax.ppermute(value, axis, [(i, (i + k) % n) for i in range(n)])]
    all_to_all x2 -> x5, starting transfers between devices: 15.6 us -> 29.6 us  [exchanged(): return lax.all_to_all(value, axis, 0, 0, tiled=True)]
    ppermute x2 -> x10, waiting for transfers between devices: 7 us -> 0.03 us  [swapped(): return lax.ppermute(value, 'c', [(0, 1), (1, 0)])]
    pallas_call x0 -> x2, Pallas kernels: none -> 4.42 us  [placed_rows(): pl.pallas_call(kernel, out_shape=jax.ShapeDtypeStruct((n_x, n_z, 2, rows,...]
    another operation x2 -> x1, other arithmetic: 4.24 us -> 0.01 us  [gathered_rows(): b_x = jnp.stack([b] + [shifted(b, 'x', k) for k in shifts[1:]])]
  transfers between devices with their start and end apart: 4 -> 27, of which waited for: 4 -> 10; matrix products, arithmetic and copies ran while one was open for 1% -> 10% of each run, Pallas kernels for 0% -> 1%
where the time goes in v2:
time: 141 us; the launch traced here: 140 us
  waiting for transfers between devices  58.5 us (41%)
  starting transfers between devices  51.9 us (37%)
  other arithmetic  14.1 us (10%)
  between operations  6.08 us (4%)
  local copies, waits for them, and re-layouts  5.4 us (4%)
  Pallas kernels  4.42 us (3%)
    all_to_all x5, waiting for transfers between devices, exchanged(): return lax.all_to_all(value, axis, 0, 0, tiled=True)  41.9 us
    all_to_all x5, starting transfers between devices, exchanged(): return lax.all_to_all(value, axis, 0, 0, tiled=True)  29.6 us
    ppermute x12, waiting for transfers between devices, shifted(): return lax.ppermute(value, axis, [(i, (i + k) % n) for i in range(n)])  16.6 us
    ppermute x12, starting transfers between devices, shifted(): return lax.ppermute(value, axis, [(i, (i + k) % n) for i in range(n)])  14.6 us
    ppermute x10, starting transfers between devices, swapped(): return lax.ppermute(value, 'c', [(0, 1), (1, 0)])  7.74 us
    pallas_call x2, Pallas kernels, placed_rows(): pl.pallas_call(kernel, out_shape=jax.ShapeDtypeStruct((n_x, n_z, 2, rows,...  4.42 us
    convert_element_type x2, other arithmetic, chip_a(): sent = piece(parts, to_x, 1 - core, 0, wide)[0].astype(WIRE)  3.22 us
  transfers between devices with their start and end apart: 27, of which 10 were waited for; matrix products, arithmetic and copies ran while one was open for 10% of the time, Pallas kernels for 1%

profile of v2, /device:TPU:1, one launch (start us, length us, event | category | flops | bytes accessed | tf_op | source)
XLA Modules:
  0.0 140.4 jit_solution(17576883310053460419)
XLA Ops:
  0.7 2.0 %fusion.24 = (f16[8,8,3584]{2,1,0:T(8,128)(2,1)S(1)}, f16[8,8,3584]{2,1,0:T(8,128)(2,1)S(1)}, f16[8,8,3584]{2,1,0:T(8,128)(2,1)S(1)}) fusion(f32[4,8,2,8,4096]{4,3,2,1,0:T(8,128)} %bitcast.191, s32[]{:T(128)S(6)} %select_n.67, s32[]{:T(128)S(6)} %select_n.69, s32[]{:T(128)S(6)} %select_n.73, s32[]{:T(128)S(6)} %select_n.71), kind=kLoop, calls=%fused_computation.36 | loop fusion | flops 1376256 | bytes 4128784 | tf_op jit(solution)/shard_map/convert_element_type | solution.py:64
  2.7 3.3 %collective-permute-start.1 = (f16[8,8,3584]{2,1,0:T(8,128)(2,1)S(1)}, f16[8,8,3584]{2,1,0:T(8,128)(2,1)S(1)}, u32[]{:S(2)}, u32[]{:S(2)}) collective-permute-start(f16[8,8,3584]{2,1,0:T(8,128)(2,1)S(1)} %get-tuple-element.31), channel_id=1, source_target_pairs={{0,1},{1,0},{2,3},{3,2},{4,5},{5,4},{6,7},{7,6},{8,9},{9,8},{10,11... | collective-permute-start | bytes 1376264 | tf_op jit(solution)/shard_map/ppermute | solution.py:28
  9.5 2.3 %fusion.10 = (f16[8,8,3584]{2,1,0:T(8,128)(2,1)S(1)}, f16[8,8,3584]{2,1,0:T(8,128)(2,1)S(1)}, f16[8,8,3584]{2,1,0:T(8,128)(2,1)S(1)}) fusion(f16[8,8,3584]{2,1,0:T(8,128)(2,1)S(1)} %collective-permute-done.1, f32[4,8,2,8,4096]{4,3,2,1,0:T(8,128)} %bitcast.194, s32[]{:T(128)S(6)} %select_n.71, s32[]{:T(128)S(6)} %select_n.68, ...), kind=kLoop, calls=%fused_computation.15 | loop fusion | flops 2752512 | bytes 5505040 | tf_op jit(solution)/shard_map/convert_element_type | solution.py:67
  13.2 2.4 %collective-permute-start.6 = (f16[8,8,3584]{2,1,0:T(8,128)(2,1)S(1)}, f16[8,8,3584]{2,1,0:T(8,128)(2,1)}, u32[]{:S(2)}, u32[]{:S(2)}) collective-permute-start(f16[8,8,3584]{2,1,0:T(8,128)(2,1)S(1)} %get-tuple-element.34), channel_id=1, source_target_pairs={{0,48},{16,0},{32,16},{48,32},{1,49},{17,1},{33,17},{49,33},{2,50}... | collective-permute-start | bytes 1376264 | tf_op jit(solution)/shard_map/ppermute | solution.py:33
  17.6 8.2 %all-to-all-start.1 = ((f16[8,4,8,512]{3,2,1,0:T(8,128)(2,1)}), f16[8,4,8,512]{3,2,1,0:T(8,128)(2,1)S(1)}, u32[]{:S(2)}, u32[]{:S(2)}) async-start(f16[8,4,8,512]{3,2,1,0:T(8,128)(2,1)} %copy.81), calls=%async_computation.1 | async-start | bytes 524288 | tf_op jit(solution)/shard_map/all_to_all | solution.py:37
  25.8 9.9 %collective-permute-done.4 = f16[8,8,3584]{2,1,0:T(8,128)(2,1)S(1)} collective-permute-done((f16[8,8,3584]{2,1,0:T(8,128)(2,1)S(1)}, f16[8,8,3584]{2,1,0:T(8,128)(2,1)S(1)}, u32[]{:S(2)}, u32[]{:S(2)}) %collective-permute-start.4) | collective-permute-done | bytes 458784 | tf_op jit(solution)/shard_map/ppermute | solution.py:33
  35.7 2.5 %fusion.17 = f16[8,8,3584]{2,1,0:T(8,128)(2,1)} fusion(f16[8,8,3584]{2,1,0:T(8,128)(2,1)} %collective-permute-done.6, f16[8,8,3584]{2,1,0:T(8,128)(2,1)S(1)} %collective-permute-done.4, f16[8,8,3584]{2,1,0:T(8,128)(2,1)S(1)} %collective-permute-done.2, f16[8,8,3584]{2,1,0:T(8,128)(2,1)} %collective-permute-done, f32[4,8,2,8,4096]{4,3,2,1,0:T(8,128)} %bitcast.196, ...), kind=kLoop, calls=%fused_computation.24 | loop fusion | flops 2293760 | bytes 3211272 | tf_op jit(solution)/shard_map/convert_element_type | solution.py:77
  38.2 6.5 %all-to-all-start = ((f16[8,8,3584]{2,1,0:T(8,128)(2,1)}), f16[8,8,3584]{2,1,0:T(8,128)(2,1)S(1)}, u32[]{:S(2)}, u32[]{:S(2)}) async-start(f16[8,8,3584]{2,1,0:T(8,128)(2,1)} %fusion.17), calls=%async_computation | async-start | bytes 917504 | tf_op jit(solution)/shard_map/all_to_all | solution.py:37
  44.9 2.7 %collective-permute-start.10 = (f16[8,512]{1,0:T(8,128)(2,1)S(1)}, f16[8,512]{1,0:T(8,128)(2,1)S(1)}, u32[]{:S(2)}, u32[]{:S(2)}) collective-permute-start(f16[8,512]{1,0:T(8,128)(2,1)S(1)} %get-tuple-element.38), channel_id=1, source_target_pairs={{0,48},{16,0},{32,16},{48,32},{1,49},{17,1},{33,17},{49,33},{2,50}... | collective-permute-start | bytes 24584 | tf_op jit(solution)/shard_map/ppermute | solution.py:33
  48.9 2.7 %collective-permute-done.8 = f16[8,512]{1,0:T(8,128)(2,1)S(1)} collective-permute-done((f16[8,512]{1,0:T(8,128)(2,1)S(1)}, f16[8,512]{1,0:T(8,128)(2,1)S(1)}, u32[]{:S(2)}, u32[]{:S(2)}) %collective-permute-start.8) | collective-permute-done | bytes 8224 | tf_op jit(solution)/shard_map/ppermute | solution.py:33
  51.8 9.4 %all-to-all-done = f16[8,8,3584]{2,1,0:T(8,128)(2,1)S(1)} async-done(((f16[8,8,3584]{2,1,0:T(8,128)(2,1)}), f16[8,8,3584]{2,1,0:T(8,128)(2,1)S(1)}, u32[]{:S(2)}, u32[]{:S(2)}) %all-to-all-start) | async-done | bytes 458784 | tf_op jit(solution)/shard_map/all_to_all | solution.py:37
  62.3 8.0 %all-to-all-start.2 = ((f32[256,1,9]{2,1,0:T(1,128)}), f32[256,1,9]{2,1,0:T(1,128)S(1)}, u32[]{:S(2)}, u32[]{:S(2)}) async-start(f32[256,1,9]{2,1,0:T(1,128)} %broadcast_in_dim.6), calls=%async_computation.2 | async-start | bytes 262144 | tf_op jit(solution)/shard_map/all_to_all | solution.py:37
  71.0 12.1 %all-to-all-done.2 = f32[256,1,9]{2,1,0:T(1,128)S(1)} async-done(((f32[256,1,9]{2,1,0:T(1,128)}), f32[256,1,9]{2,1,0:T(1,128)S(1)}, u32[]{:S(2)}, u32[]{:S(2)}) %all-to-all-start.2) | async-done | bytes 9248 | tf_op jit(solution)/shard_map/all_to_all | solution.py:37
  87.9 3.5 %all-to-all-start.3 = ((bf16[8,8,3072]{2,1,0:T(8,128)(2,1)}), bf16[8,8,3072]{2,1,0:T(8,128)(2,1)S(1)}, u32[]{:S(2)}, u32[]{:S(2)}) async-start(bf16[8,8,3072]{2,1,0:T(8,128)(2,1)} %broadcast_in_dim.7), calls=%async_computation.3 | async-start | bytes 786432 | tf_op jit(solution)/shard_map/all_to_all | solution.py:37
  92.6 2.2 %collective-permute-start.20 = (bf16[8,1024]{1,0:T(8,128)(2,1)S(1)}, bf16[8,1024]{1,0:T(8,128)(2,1)S(1)}, u32[]{:S(2)}, u32[]{:S(2)}) collective-permute-start(bf16[8,1024]{1,0:T(8,128)(2,1)S(1)} %get-tuple-element.36), channel_id=1, source_target_pairs={{0,48},{16,0},{32,16},{48,32},{1,49},{17,1},{33,17},{49,33},{2,50}... | collective-permute-start | bytes 49160 | tf_op jit(solution)/shard_map/ppermute | solution.py:33
  95.9 9.8 %all-to-all-done.3.refs_1_ = bf16[8,8,3072]{2,1,0:T(8,128)(2,1)S(1)} async-done(((bf16[8,8,3072]{2,1,0:T(8,128)(2,1)}), bf16[8,8,3072]{2,1,0:T(8,128)(2,1)S(1)}, u32[]{:S(2)}, u32[]{:S(2)}) %all-to-all-start.3) | async-done | bytes 393248 | tf_op jit(solution)/shard_map/all_to_all | solution.py:37
  106.6 3.5 %all-to-all-start.4 = ((bf16[8,4,8,1024]{3,2,1,0:T(8,128)(2,1)}), bf16[8,4,8,1024]{3,2,1,0:T(8,128)(2,1)S(1)}, u32[]{:S(2)}, u32[]{:S(2)}) async-start(bf16[8,4,8,1024]{3,2,1,0:T(8,128)(2,1)} %broadcast_in_dim.8), calls=%async_computation.4 | async-start | bytes 1048576 | tf_op jit(solution)/shard_map/all_to_all | solution.py:37
  110.1 1.4 %collective-permute-start.12 = (bf16[8,8,3072]{2,1,0:T(8,128)(2,1)S(1)}, bf16[8,8,3072]{2,1,0:T(8,128)(2,1)S(1)}, u32[]{:S(2)}, u32[]{:S(2)}) collective-permute-start(bf16[8,8,3072]{2,1,0:T(8,128)(2,1)S(1)} %all-to-all-done.3.refs_1_), channel_id=1, source_target_pairs={{0,32},{16,48},{32,0},{48,16},{1,33},{17,49},{33,1},{49,17},{2,34}... | collective-permute-start | bytes 1179656 | tf_op jit(solution)/shard_map/ppermute | solution.py:33
  111.5 2.7 %collective-permute-start.16 = (bf16[8,8,3072]{2,1,0:T(8,128)(2,1)S(1)}, bf16[8,8,3072]{2,1,0:T(8,128)(2,1)S(1)}, u32[]{:S(2)}, u32[]{:S(2)}) collective-permute-start(bf16[8,8,3072]{2,1,0:T(8,128)(2,1)S(1)} %all-to-all-done.3.refs_1_), channel_id=1, source_target_pairs={{0,48},{16,0},{32,16},{48,32},{1,49},{17,1},{33,17},{49,33},{2,50}... | collective-permute-start | bytes 1179656 | tf_op jit(solution)/shard_map/ppermute | solution.py:33
  116.4 10.6 %all-to-all-done.4.refs_5_ = bf16[8,4,8,1024]{3,2,1,0:T(8,128)(2,1)S(1)} async-done(((bf16[8,4,8,1024]{3,2,1,0:T(8,128)(2,1)}), bf16[8,4,8,1024]{3,2,1,0:T(8,128)(2,1)S(1)}, u32[]{:S(2)}, u32[]{:S(2)}) %all-to-all-start.4) | async-done | bytes 524320 | tf_op jit(solution)/shard_map/all_to_all | solution.py:37
  128.4 2.7 %collective-permute-done.14.refs_3_ = bf16[8,8,3072]{2,1,0:T(8,128)(2,1)S(1)} collective-permute-done((bf16[8,8,3072]{2,1,0:T(8,128)(2,1)S(1)}, bf16[8,8,3072]{2,1,0:T(8,128)(2,1)S(1)}, u32[]{:S(2)}, u32[]{:S(2)}) %collective-permute-start.14) | collective-permute-done | bytes 393248 | tf_op jit(solution)/shard_map/ppermute | solution.py:33
  131.6 1.8 %multiply_subtract_fusion = (f32[1,8,4096]{2,1,0:T(8,128)}, f32[1,8,4096]{2,1,0:T(8,128)}, f32[1,8,4096]{2,1,0:T(8,128)}) fusion(f32[1,8,4096]{2,1,0:T(8,128)} %param.9, f32[]{:T(128)} %bitcast.29, f32[]{:T(128)} %bitcast.27, f32[]{:T(128)S(6)} %multiply.17, f32[1,8,512]{2,1,0:T(8,128)S(1)} %bitcast.199, f32[1,8,3584]{2,1,0:T(8,128)S(1)} %bitcast.197, ...), kind=kLoop, calls=%fused_computation.60 | loop fusion | flops 589824 | bytes 917516 | tf_op jit(solution)/shard_map/sub | solution.py:176
  134.8 1.9 %shard_map.118.refs_6_ = bf16[4,8,2,8,4096]{4,3,2,1,0:T(8,128)(2,1)} custom-call(s32[5]{0:T(128)S(1)} %stack.55.refs_0_, bf16[8,8,3072]{2,1,0:T(8,128)(2,1)S(1)} %all-to-all-done.3.refs_1_, bf16[8,8,3072]{2,1,0:T(8,128)(2,1)S(1)} %collective-permute-done.12.refs_2_, bf16[8,8,3072]{2,1,0:T(8,128)(2,1)S(1)} %collective-permute-done.14.refs_3_, ...), custom_call_target="tpu_custom_call" | custom-call | tf_op jit(solution)/shard_map/pallas_call | solution.py:109
  136.8 2.5 %shard_map.119 = bf16[4,8,2,8,4096]{4,3,2,1,0:T(8,128)(2,1)} custom-call(s32[5]{0:T(128)S(1)} %stack.48.refs_0_, bf16[8,8,3072]{2,1,0:T(8,128)(2,1)S(1)} %collective-permute-done.11.refs_1_, bf16[8,8,3072]{2,1,0:T(8,128)(2,1)S(1)} %collective-permute-done.13.refs_2_, ...), custom_call_target="tpu_custom_call", output_to_operand_aliasing={{}: (6, {})} | custom-call | tf_op jit(solution)/shard_map/pallas_call | solution.py:109
  (74 shorter events, 20.0 us)
Async XLA Ops:
  2.7 6.8 %collective-permute-start.1 = (f16[8,8,3584]{2,1,0:T(8,128)(2,1)S(1)}, f16[8,8,3584]{2,1,0:T(8,128)(2,1)S(1)}, u32[]{:S(2)}, u32[]{:S(2)}) collective-permute-start(f16[8,8,3584]{2,1,0:T(8,128)(2,1)S(1)} %get-tuple-element.31), channel_id=1, source_target_pairs={{0,1},{1,0},{2,3},{3,2},{4,5},{5,4},{6,7},{7,6},{8,9},{9,8},{10,11... | collective-permute-start | bytes 1376264 | tf_op jit(solution)/shard_map/ppermute | solution.py:28
  7.8 17.9 %collective-permute-start = (f16[8,8,3584]{2,1,0:T(8,128)(2,1)S(1)}, f16[8,8,3584]{2,1,0:T(8,128)(2,1)}, u32[]{:S(2)}, u32[]{:S(2)}) collective-permute-start(f16[8,8,3584]{2,1,0:T(8,128)(2,1)S(1)} %get-tuple-element.29), channel_id=1, source_target_pairs={{0,1},{1,0},{2,3},{3,2},{4,5},{5,4},{6,7},{7,6},{8,9},{9,8},{10,11... | collective-permute-start | bytes 1376264 | tf_op jit(solution)/shard_map/ppermute | solution.py:28
  9.0 6.6 %collective-permute-start.7 = (f16[4,8,8,512]{3,2,1,0:T(8,128)(2,1)S(1)}, f16[4,8,8,512]{3,2,1,0:T(8,128)(2,1)}, u32[]{:S(2)}, u32[]{:S(2)}) collective-permute-start(f16[4,8,8,512]{3,2,1,0:T(8,128)(2,1)S(1)} %fusion.27), channel_id=1, source_target_pairs={{0,1},{1,0},{2,3},{3,2},{4,5},{5,4},{6,7},{7,6},{8,9},{9,8},{10,11... | collective-permute-start | bytes 786440 | tf_op jit(solution)/shard_map/ppermute | solution.py:28
  11.8 14.0 %collective-permute-start.2 = (f16[8,8,3584]{2,1,0:T(8,128)(2,1)S(1)}, f16[8,8,3584]{2,1,0:T(8,128)(2,1)S(1)}, u32[]{:S(2)}, u32[]{:S(2)}) collective-permute-start(f16[8,8,3584]{2,1,0:T(8,128)(2,1)S(1)} %get-tuple-element.32), channel_id=1, source_target_pairs={{0,32},{16,48},{32,0},{48,16},{1,33},{17,49},{33,1},{49,17},{2,34}... | collective-permute-start | bytes 1376264 | tf_op jit(solution)/shard_map/ppermute | solution.py:33
  12.9 22.7 %collective-permute-start.4 = (f16[8,8,3584]{2,1,0:T(8,128)(2,1)S(1)}, f16[8,8,3584]{2,1,0:T(8,128)(2,1)S(1)}, u32[]{:S(2)}, u32[]{:S(2)}) collective-permute-start(f16[8,8,3584]{2,1,0:T(8,128)(2,1)S(1)} %get-tuple-element.33), channel_id=1, source_target_pairs={{0,16},{16,32},{32,48},{48,0},{1,17},{17,33},{33,49},{49,1},{2,18}... | collective-permute-start | bytes 1376264 | tf_op jit(solution)/shard_map/ppermute | solution.py:33
  13.2 22.4 %collective-permute-start.6 = (f16[8,8,3584]{2,1,0:T(8,128)(2,1)S(1)}, f16[8,8,3584]{2,1,0:T(8,128)(2,1)}, u32[]{:S(2)}, u32[]{:S(2)}) collective-permute-start(f16[8,8,3584]{2,1,0:T(8,128)(2,1)S(1)} %get-tuple-element.34), channel_id=1, source_target_pairs={{0,48},{16,0},{32,16},{48,32},{1,49},{17,1},{33,17},{49,33},{2,50}... | collective-permute-start | bytes 1376264 | tf_op jit(solution)/shard_map/ppermute | solution.py:33
  17.6 20.6 %all-to-all-start.1 = ((f16[8,4,8,512]{3,2,1,0:T(8,128)(2,1)}), f16[8,4,8,512]{3,2,1,0:T(8,128)(2,1)S(1)}, u32[]{:S(2)}, u32[]{:S(2)}) async-start(f16[8,4,8,512]{3,2,1,0:T(8,128)(2,1)} %copy.81), calls=%async_computation.1 | async-start | bytes 524288 | tf_op jit(solution)/shard_map/all_to_all | solution.py:37
  38.2 22.9 %all-to-all-start = ((f16[8,8,3584]{2,1,0:T(8,128)(2,1)}), f16[8,8,3584]{2,1,0:T(8,128)(2,1)S(1)}, u32[]{:S(2)}, u32[]{:S(2)}) async-start(f16[8,8,3584]{2,1,0:T(8,128)(2,1)} %fusion.17), calls=%async_computation | async-start | bytes 917504 | tf_op jit(solution)/shard_map/all_to_all | solution.py:37
  44.9 4.0 %collective-permute-start.10 = (f16[8,512]{1,0:T(8,128)(2,1)S(1)}, f16[8,512]{1,0:T(8,128)(2,1)S(1)}, u32[]{:S(2)}, u32[]{:S(2)}) collective-permute-start(f16[8,512]{1,0:T(8,128)(2,1)S(1)} %get-tuple-element.38), channel_id=1, source_target_pairs={{0,48},{16,0},{32,16},{48,32},{1,49},{17,1},{33,17},{49,33},{2,50}... | collective-permute-start | bytes 24584 | tf_op jit(solution)/shard_map/ppermute | solution.py:33
  47.5 4.0 %collective-permute-start.8 = (f16[8,512]{1,0:T(8,128)(2,1)S(1)}, f16[8,512]{1,0:T(8,128)(2,1)S(1)}, u32[]{:S(2)}, u32[]{:S(2)}) collective-permute-start(f16[8,512]{1,0:T(8,128)(2,1)S(1)} %get-tuple-element.37), channel_id=1, source_target_pairs={{0,32},{16,48},{32,0},{48,16},{1,33},{17,49},{33,1},{49,17},{2,34}... | collective-permute-start | bytes 24584 | tf_op jit(solution)/shard_map/ppermute | solution.py:33
  48.0 3.7 %collective-permute-start.9 = (f16[8,512]{1,0:T(8,128)(2,1)S(1)}, f16[8,512]{1,0:T(8,128)(2,1)S(1)}, u32[]{:S(2)}, u32[]{:S(2)}) collective-permute-start(f16[8,512]{1,0:T(8,128)(2,1)S(1)} %get-tuple-element.39), channel_id=1, source_target_pairs={{0,16},{16,32},{32,48},{48,0},{1,17},{17,33},{33,49},{49,1},{2,18}... | collective-permute-start | bytes 24584 | tf_op jit(solution)/shard_map/ppermute | solution.py:33
  62.3 20.8 %all-to-all-start.2 = ((f32[256,1,9]{2,1,0:T(1,128)}), f32[256,1,9]{2,1,0:T(1,128)S(1)}, u32[]{:S(2)}, u32[]{:S(2)}) async-start(f32[256,1,9]{2,1,0:T(1,128)} %broadcast_in_dim.6), calls=%async_computation.2 | async-start | bytes 262144 | tf_op jit(solution)/shard_map/all_to_all | solution.py:37
  87.9 17.8 %all-to-all-start.3 = ((bf16[8,8,3072]{2,1,0:T(8,128)(2,1)}), bf16[8,8,3072]{2,1,0:T(8,128)(2,1)S(1)}, u32[]{:S(2)}, u32[]{:S(2)}) async-start(bf16[8,8,3072]{2,1,0:T(8,128)(2,1)} %broadcast_in_dim.7), calls=%async_computation.3 | async-start | bytes 786432 | tf_op jit(solution)/shard_map/all_to_all | solution.py:37
  91.4 4.2 %collective-permute-start.18 = (bf16[8,1024]{1,0:T(8,128)(2,1)S(1)}, bf16[8,1024]{1,0:T(8,128)(2,1)S(1)}, u32[]{:S(2)}, u32[]{:S(2)}) collective-permute-start(bf16[8,1024]{1,0:T(8,128)(2,1)S(1)} %get-tuple-element.36), channel_id=1, source_target_pairs={{0,32},{16,48},{32,0},{48,16},{1,33},{17,49},{33,1},{49,17},{2,34}... | collective-permute-start | bytes 49160 | tf_op jit(solution)/shard_map/ppermute | solution.py:33
  92.1 3.8 %collective-permute-start.19 = (bf16[8,1024]{1,0:T(8,128)(2,1)S(1)}, bf16[8,1024]{1,0:T(8,128)(2,1)S(1)}, u32[]{:S(2)}, u32[]{:S(2)}) collective-permute-start(bf16[8,1024]{1,0:T(8,128)(2,1)S(1)} %get-tuple-element.36), channel_id=1, source_target_pairs={{0,16},{16,32},{32,48},{48,0},{1,17},{17,33},{33,49},{49,1},{2,18}... | collective-permute-start | bytes 49160 | tf_op jit(solution)/shard_map/ppermute | solution.py:33
  106.6 20.5 %all-to-all-start.4 = ((bf16[8,4,8,1024]{3,2,1,0:T(8,128)(2,1)}), bf16[8,4,8,1024]{3,2,1,0:T(8,128)(2,1)S(1)}, u32[]{:S(2)}, u32[]{:S(2)}) async-start(bf16[8,4,8,1024]{3,2,1,0:T(8,128)(2,1)} %broadcast_in_dim.8), calls=%async_computation.4 | async-start | bytes 1048576 | tf_op jit(solution)/shard_map/all_to_all | solution.py:37
  110.1 18.4 %collective-permute-start.12 = (bf16[8,8,3072]{2,1,0:T(8,128)(2,1)S(1)}, bf16[8,8,3072]{2,1,0:T(8,128)(2,1)S(1)}, u32[]{:S(2)}, u32[]{:S(2)}) collective-permute-start(bf16[8,8,3072]{2,1,0:T(8,128)(2,1)S(1)} %all-to-all-done.3.refs_1_), channel_id=1, source_target_pairs={{0,32},{16,48},{32,0},{48,16},{1,33},{17,49},{33,1},{49,17},{2,34}... | collective-permute-start | bytes 1179656 | tf_op jit(solution)/shard_map/ppermute | solution.py:33
  111.5 19.6 %collective-permute-start.14 = (bf16[8,8,3072]{2,1,0:T(8,128)(2,1)S(1)}, bf16[8,8,3072]{2,1,0:T(8,128)(2,1)S(1)}, u32[]{:S(2)}, u32[]{:S(2)}) collective-permute-start(bf16[8,8,3072]{2,1,0:T(8,128)(2,1)S(1)} %all-to-all-done.3.refs_1_), channel_id=1, source_target_pairs={{0,16},{16,32},{32,48},{48,0},{1,17},{17,33},{33,49},{49,1},{2,18}... | collective-permute-start | bytes 1179656 | tf_op jit(solution)/shard_map/ppermute | solution.py:33
  111.5 20.1 %collective-permute-start.16 = (bf16[8,8,3072]{2,1,0:T(8,128)(2,1)S(1)}, bf16[8,8,3072]{2,1,0:T(8,128)(2,1)S(1)}, u32[]{:S(2)}, u32[]{:S(2)}) collective-permute-start(bf16[8,8,3072]{2,1,0:T(8,128)(2,1)S(1)} %all-to-all-done.3.refs_1_), channel_id=1, source_target_pairs={{0,48},{16,0},{32,16},{48,32},{1,49},{17,1},{33,17},{49,33},{2,50}... | collective-permute-start | bytes 1179656 | tf_op jit(solution)/shard_map/ppermute | solution.py:33
  115.1 21.6 %collective-permute-start.11 = (bf16[8,8,3072]{2,1,0:T(8,128)(2,1)S(1)}, bf16[8,8,3072]{2,1,0:T(8,128)(2,1)S(1)}, u32[]{:S(2)}, u32[]{:S(2)}) collective-permute-start(bf16[8,8,3072]{2,1,0:T(8,128)(2,1)S(1)} %all-to-all-done.3.refs_1_), channel_id=1, source_target_pairs={{0,1},{1,0},{2,3},{3,2},{4,5},{5,4},{6,7},{7,6},{8,9},{9,8},{10,11... | collective-permute-start | bytes 1179656 | tf_op jit(solution)/shard_map/ppermute | solution.py:28
  127.0 9.7 %collective-permute-start.21 = (bf16[8,4,8,1024]{3,2,1,0:T(8,128)(2,1)S(1)}, bf16[8,4,8,1024]{3,2,1,0:T(8,128)(2,1)S(1)}, u32[]{:S(2)}, u32[]{:S(2)}) collective-permute-start(bf16[8,4,8,1024]{3,2,1,0:T(8,128)(2,1)S(1)} %all-to-all-done.4.refs_5_), channel_id=1, source_target_pairs={{0,1},{1,0},{2,3},{3,2},{4,5},{5,4},{6,7},{7,6},{8,9},{9,8},{10,11... | collective-permute-start | bytes 1572872 | tf_op jit(solution)/shard_map/ppermute | solution.py:28
  128.4 8.3 %collective-permute-start.13 = (bf16[8,8,3072]{2,1,0:T(8,128)(2,1)S(1)}, bf16[8,8,3072]{2,1,0:T(8,128)(2,1)S(1)}, u32[]{:S(2)}, u32[]{:S(2)}) collective-permute-start(bf16[8,8,3072]{2,1,0:T(8,128)(2,1)S(1)} %collective-permute-done.12.refs_2_), channel_id=1, source_target_pairs={{0,1},{1,0},{2,3},{3,2},{4,5},{5,4},{6,7},{7,6},{8,9},{9,8},{10,11... | collective-permute-start | bytes 1179656 | tf_op jit(solution)/shard_map/ppermute | solution.py:28
  131.1 5.6 %collective-permute-start.15 = (bf16[8,8,3072]{2,1,0:T(8,128)(2,1)S(1)}, bf16[8,8,3072]{2,1,0:T(8,128)(2,1)}, u32[]{:S(2)}, u32[]{:S(2)}) collective-permute-start(bf16[8,8,3072]{2,1,0:T(8,128)(2,1)S(1)} %collective-permute-done.14.refs_3_), channel_id=1, source_target_pairs={{0,1},{1,0},{2,3},{3,2},{4,5},{5,4},{6,7},{7,6},{8,9},{9,8},{10,11... | collective-permute-start | bytes 1179656 | tf_op jit(solution)/shard_map/ppermute | solution.py:28
  131.6 5.2 %collective-permute-start.17 = (bf16[8,8,3072]{2,1,0:T(8,128)(2,1)S(1)}, bf16[8,8,3072]{2,1,0:T(8,128)(2,1)}, u32[]{:S(2)}, u32[]{:S(2)}) collective-permute-start(bf16[8,8,3072]{2,1,0:T(8,128)(2,1)S(1)} %collective-permute-done.16.refs_4_), channel_id=1, source_target_pairs={{0,1},{1,0},{2,3},{3,2},{4,5},{5,4},{6,7},{7,6},{8,9},{9,8},{10,11... | collective-permute-start | bytes 1179656 | tf_op jit(solution)/shard_map/ppermute | solution.py:28
  (7 other events, 306.1 us)

commit v3 on v2

v3 whole, which is shorter than its diff:
```python
import jax
import jax.numpy as jnp
from jax import lax
from jax.experimental import pallas as pl
from jax.experimental.pallas import tpu as pltpu
from jax.sharding import Mesh
from jax.sharding import PartitionSpec as P


MICRO = 32
DP = ("x", "z", "c")
ALL = ("section", "x", "z", "c")

beta_one = 0.9
beta_two = 0.95
learn_rate = 0.05
weight_decay = 0.1
epsilon = 1e-08

WIRE = jnp.float16
SCALE = 0.5

SUM_SHARE = 14
GATHER_SHARE = 13


def swapped(value):
    return lax.ppermute(value, "c", [(0, 1), (1, 0)])


def shifted(value, axis, k):
    n = lax.axis_size(axis)
    return lax.ppermute(value, axis, [(i, (i + k) % n) for i in range(n)])


def exchanged(value, axis):
    return lax.all_to_all(value, axis, 0, 0, tiled=True)


def hops(n):
    return sorted(range(1, n), key=lambda k: -min(k, n - k))


def piece(parts, at_x, core, first, width):
    n_x, n_z, _, rows, _ = parts.shape
    start = (0 if at_x is None else at_x, 0, core, 0, first)
    taken = (n_x if at_x is None else 1, n_z, 1, rows, width)
    return lax.dynamic_slice(parts, start, taken)[:, :, 0] * SCALE


def at(values, i):
    return lax.dynamic_index_in_dim(values, i, 0, keepdims=False).astype(jnp.float32)


def after(value, *others):
    return lax.optimization_barrier((value, *others))[0]


def reduced_rows(flat, own_rows):
    n_x, n_z, n_c = (lax.axis_size(a) for a in DP)
    x, core = lax.axis_index("x"), lax.axis_index("c")
    width = flat.shape[1]
    parts = flat.reshape(n_x, n_z, n_c, own_rows, width)
    wide = width * SUM_SHARE // 16

    def encoded(source, k):
        return piece(source, (x + k) % n_x, 1 - core, 0, wide)[0].astype(WIRE)

    def summed_chip(source, k, other):
        return piece(source, (x + k) % n_x, core, 0, wide)[0] + other.astype(jnp.float32)

    order = hops(n_x)
    sent = [encoded(parts, k) for k in order]
    sent_b = piece(after(parts, *sent), None, 1 - core, wide, width - wide).astype(WIRE)
    other = [swapped(v) for v in sent]
    other_b = swapped(sent_b)
    chips = [
        summed_chip(parts, k, v).astype(WIRE) for k, v in zip(order, other, strict=True)
    ]
    arrived = [shifted(v, "x", k) for k, v in zip(order, chips, strict=True)]
    late = after(parts, *chips)
    chip_b = piece(late, None, core, wide, width - wide)
    chip_b = chip_b + other_b.astype(jnp.float32)
    chip_b = chip_b.transpose(1, 0, 2, 3).astype(WIRE)
    b_z = exchanged(chip_b, "z")
    b_z = b_z.astype(jnp.float32).sum(axis=0)
    late = after(parts, chip_b)
    own = encoded(late, 0)
    own = swapped(own)
    a_x = lax.optimization_barrier(summed_chip(late, 0, own))
    for value in arrived:
        a_x = a_x + value.astype(jnp.float32)
    b_sent = [shifted(at(b_z, (x + k) % n_x).astype(WIRE), "x", k) for k in hops(n_x)]
    a_z = exchanged(a_x.astype(WIRE), "z").astype(jnp.float32).sum(axis=0)
    b_x = at(b_z, x)
    for value in b_sent:
        b_x = b_x + value.astype(jnp.float32)
    return jnp.concatenate([a_z, b_x], axis=1) * (1.0 / SCALE)


def stepped(summed, good, clip, moment_one, moment_two, master, fix_one, fix_two):
    clipped = summed / good / clip
    first_next = beta_one * moment_one + (1.0 - beta_one) * clipped
    second_next = beta_two * moment_two + (1.0 - beta_two) * clipped * clipped
    update = first_next / fix_one / (jnp.sqrt(second_next / fix_two) + epsilon)
    master_next = master - learn_rate * (update + weight_decay * master)
    return master_next, first_next, second_next


def normed_rows(reports, summed, moment_one, moment_two, master, section, fixes, sizes):
    n_section, n_z, wide, elements = sizes
    rows, width = summed.shape
    columns = reports.shape[-1]
    each = reports.shape[0] // n_section

    def kernel(section, fixes, reports, summed, one, two, master, a, b, facts):
        sums = [
            jnp.sum(reports[pl.ds(i * each, each)], axis=0) for i in range(n_section)
        ]
        good = sums[0][:, columns - 1 :]
        squares = [v / (good * good) for v in sums]
        own, total = squares[0], squares[0]
        for i in range(1, n_section):
            own = jnp.where(section[0] == i, squares[i], own)
            total = total + squares[i]
        lane = lax.broadcasted_iota(jnp.int32, total.shape, 1)
        total = jnp.where(lane < columns - 1, total, 0.0)
        norm = jnp.sqrt(jnp.sum(total, axis=1, keepdims=True) / elements)
        clip = jnp.maximum(1.0, norm)
        facts[0:1] = own
        for i, value in enumerate((good, clip, norm)):
            facts[i + 1 : i + 2] = jnp.broadcast_to(value, own.shape)
        master_next = stepped(
            summed[...], good, clip, one[...], two[...], master[...], fixes[0], fixes[1]
        )[0]
        sent = master_next.astype(a.dtype)
        a[...] = jnp.broadcast_to(sent[None, :, :wide], a.shape)
        b[...] = sent[:, wide:]

    scalar = pl.BlockSpec(memory_space=pltpu.SMEM)
    near = pl.BlockSpec(memory_space=pltpu.VMEM)
    return pl.pallas_call(
        kernel,
        out_shape=(
            jax.ShapeDtypeStruct((n_z, rows, wide), jnp.bfloat16),
            jax.ShapeDtypeStruct((rows, width - wide), jnp.bfloat16),
            jax.ShapeDtypeStruct((4, columns), jnp.float32),
        ),
        in_specs=[scalar] * 2 + [near] * 5,
        out_specs=(near, near, near),
        compiler_params=pltpu.CompilerParams(vmem_limit_bytes=8 << 20),
    )(section, fixes, reports, summed, moment_one, moment_two, master)


def placed_rows(shape, spots, pieces, out=None):
    total = sum(1 if axis is None else v.shape[axis] for v, axis, _ in pieces)

    def kernel(*refs):
        spots, ins, to, sems = refs[0], refs[1 : 1 + len(pieces)], refs[-2], refs[-1]
        copies = []
        for ref, (_, axis, first) in zip(ins, pieces, strict=True):
            views = [ref]
            if axis is not None:
                views = [ref.at[:, j] for j in range(ref.shape[axis])]
            for view in views:
                i = len(copies)
                columns = pl.ds(first, view.shape[-1])
                there = to.at[spots[2 * i], :, spots[2 * i + 1], :, columns]
                copies.append(pltpu.make_async_copy(view, there, sems.at[i]))
        for copy in copies:
            copy.start()
        for copy in copies:
            copy.wait()

    near = pl.BlockSpec(memory_space=pltpu.VMEM)
    far = pl.BlockSpec(memory_space=pltpu.HBM)
    operands = [spots, *(v for v, _, _ in pieces)] + ([] if out is None else [out])
    specs = [pl.BlockSpec(memory_space=pltpu.SMEM)] + [near] * len(pieces)
    return pl.pallas_call(
        kernel,
        out_shape=jax.ShapeDtypeStruct(shape, pieces[0][0].dtype),
        in_specs=specs + [far] * (len(operands) - len(specs)),
        out_specs=far,
        scratch_shapes=[pltpu.SemaphoreType.DMA((total,))],
        input_output_aliases={} if out is None else {len(operands) - 1: 0},
        compiler_params=pltpu.CompilerParams(vmem_limit_bytes=8 << 20),
    )(*operands)


def gathered_rows(a, b):
    n_x, n_z, n_c = (lax.axis_size(a) for a in DP)
    x, core = lax.axis_index("x"), lax.axis_index("c")
    own_rows, width = b.shape[0], a.shape[2] + b.shape[1]
    shifts = [0] + hops(n_x)
    b_x = [b] + [shifted(b, "x", k) for k in shifts[1:]]
    b_x = jnp.stack(b_x)
    b_x = jnp.broadcast_to(b_x[None], (n_z, *b_x.shape))
    a_z = exchanged(a, "z")
    a_all = [a_z, shifted(a_z, "x", shifts[1])]
    a_all += [shifted(a_z, "x", k) for k in shifts[2:]]
    b_all = exchanged(b_x, "z")
    a_other = [swapped(v) for v in a_all]
    b_other = swapped(b_all)
    origin = [lax.rem(x + (n_x - k), n_x) for k in shifts]
    wide = a.shape[2]
    shape = (n_x, n_z, n_c, own_rows, width)

    def spots(*pairs):
        return jnp.stack([v for pair in pairs for v in pair])

    out = placed_rows(
        shape,
        spots(*((origin[j], c) for j in (0, 1) for c in (core, 1 - core))),
        [(v[j], None, 0) for j in (0, 1) for v in (a_all, a_other)],
    )
    for a_last, b_last, c in ((a_all, b_all, core), (a_other, b_other, 1 - core)):
        out = placed_rows(
            shape,
            spots(*((origin[j], c) for j in range(2, n_x)), *((o, c) for o in origin)),
            [(v, None, 0) for v in a_last[2:]] + [(b_last, 1, wide)],
            out,
        )
    return out.reshape(n_x * n_z * n_c * own_rows, width)


def on_device(grads, skipped, master, moment_one, moment_two, bounds, step):
    flat_grads = grads[0, 0]
    rows_all, width = flat_grads.shape
    own_rows = master.shape[1]
    layers = bounds.shape[1] - 1
    n_section = lax.axis_size("section")
    n_all = lax.axis_size(ALL)
    summed = reduced_rows(flat_grads, own_rows)

    row_index = lax.axis_index(DP) * own_rows + jnp.arange(own_rows, dtype=jnp.int32)
    inside = (row_index[:, None] >= bounds[0, None, :-1]) & (
        row_index[:, None] < bounds[0, None, 1:]
    )
    row_squares = jnp.sum(summed * summed, axis=1)
    layer_part = jnp.sum(row_squares[:, None] * inside.astype(jnp.float32), axis=0)
    good = (MICRO - skipped).astype(jnp.float32)
    report = jnp.concatenate([layer_part, good])
    reports = exchanged(jnp.broadcast_to(report, (n_all, 1, layers + 1)), ALL)
    step_value = step[0].astype(jnp.float32)
    fix_one = 1.0 - jnp.power(beta_one, step_value)
    fix_two = 1.0 - jnp.power(beta_two, step_value)
    state = (moment_one[0], moment_two[0], master[0])
    sizes = (
        n_section,
        lax.axis_size("z"),
        width * GATHER_SHARE // 16,
        n_section * rows_all * width,
    )
    a, b, facts = normed_rows(
        reports,
        summed,
        *state,
        lax.axis_index("section").reshape(1),
        jnp.stack([fix_one, fix_two]),
        sizes,
    )
    gathered = gathered_rows(a, b)
    good, clip, grad_rms = facts[1, 0], facts[2, 0], facts[3, 0]
    layer_rows = (bounds[0, 1:] - bounds[0, :-1]).astype(jnp.float32)
    layer_norms = jnp.sqrt(facts[0, :layers] / (layer_rows * width))
    master_next, first_next, second_next = stepped(
        summed, good, clip, *state, fix_one, fix_two
    )
    return (
        gathered[None],
        master_next[None],
        first_next[None],
        second_next[None],
        layer_norms[None],
        grad_rms.reshape(1),
    )


def solution(mesh):
    split = Mesh(
        mesh.devices.reshape(mesh.shape["section"], 4, 8, 2), ("section", "x", "z", "c")
    )
    placed = (
        P("section", DP, None, None),
        P(DP),
        P("section", DP, None),
        P("section", DP, None),
        P("section", DP, None),
        P("section", None),
        P(),
    )

    return jax.shard_map(
        on_device,
        mesh=split,
        in_specs=placed,
        out_specs=(
            P("section", None, None),
            P("section", DP, None),
            P("section", DP, None),
            P("section", DP, None),
            P("section", None),
            P(),
        ),
        check_vma=False,
    )
```

time: 141 us -> 140 us (level)
  waiting for transfers between devices: 58.5 us -> 62.9 us
  starting transfers between devices: 51.9 us -> 48.9 us
  between operations: 6.08 us -> 3.71 us
  local copies, waits for them, and re-layouts: 5.4 us -> 3.13 us
  Pallas kernels: 4.42 us -> 6.67 us
    ppermute x12, waiting for transfers between devices: 16.6 us -> 19.4 us  [shifted(): return lax.ppermute(value, axis, [(i, (i + k) % n) for i in range(n)])]
    pallas_call x2 -> x4, Pallas kernels: 4.42 us -> 6.67 us  [the longest x3 5 us: placed_rows(): pl.pallas_call(kernel, out_shape=jax.ShapeDtypeStruct(shape, pieces[0][0]...]
    ppermute x10, starting transfers between devices: 7.74 us -> 5.87 us  [swapped(): return lax.ppermute(value, 'c', [(0, 1), (1, 0)])]
    convert_element_type x5, other arithmetic: 6.71 us -> 8.3 us  [the longest x2 3.23 us: encoded(): return piece(source, (x + k) % n_x, 1 - core, 0, wide)[0].astype(WIRE)]
    add x0 -> x1, other arithmetic: none -> 1.44 us  [summed_chip(): piece(source, (x + k) % n_x, core, 0, wide)[0] + other.astype(jnp.float32)]
    unnamed x12 -> x8, local copies, waits for them, and re-layouts: 1.45 us -> 0.02 us
  transfers between devices with their start and end apart: 27 -> 27, of which waited for: 10 -> 11; matrix products, arithmetic and copies ran while one was open for 10% -> 8% of each run, Pallas kernels for 1% -> 2%
where the time goes in v3:
time: 140 us; the launch traced here: 139 us
  waiting for transfers between devices  62.9 us (45%)
  starting transfers between devices  48.9 us (35%)
  other arithmetic  13.9 us (10%)
  Pallas kernels  6.67 us (5%)
  between operations  3.71 us (3%)
  local copies, waits for them, and re-layouts  3.13 us (2%)
    all_to_all x5, waiting for transfers between devices, exchanged(): return lax.all_to_all(value, axis, 0, 0, tiled=True)  43.1 us
    all_to_all x5, starting transfers between devices, exchanged(): return lax.all_to_all(value, axis, 0, 0, tiled=True)  29.3 us
    ppermute x12, waiting for transfers between devices, shifted(): return lax.ppermute(value, axis, [(i, (i + k) % n) for i in range(n)])  19.4 us
    ppermute x12, starting transfers between devices, shifted(): return lax.ppermute(value, axis, [(i, (i + k) % n) for i in range(n)])  13.7 us
    ppermute x10, starting transfers between devices, swapped(): return lax.ppermute(value, 'c', [(0, 1), (1, 0)])  5.87 us
    pallas_call x3, Pallas kernels, placed_rows(): pl.pallas_call(kernel, out_shape=jax.ShapeDtypeStruct(shape, pieces[0][0]...  5 us
    convert_element_type x2, other arithmetic, encoded(): return piece(source, (x + k) % n_x, 1 - core, 0, wide)[0].astype(WIRE)  3.23 us
  transfers between devices with their start and end apart: 27, of which 11 were waited for; matrix products, arithmetic and copies ran while one was open for 8% of the time, Pallas kernels for 2%

profile of v3, /device:TPU:1, one launch (start us, length us, event | category | flops | bytes accessed | tf_op | source)
XLA Modules:
  0.0 139.2 jit_solution(11486068230048732848)
XLA Ops:
  0.7 2.0 %fusion.18 = (f16[8,8,3584]{2,1,0:T(8,128)(2,1)S(1)}, f16[8,8,3584]{2,1,0:T(8,128)(2,1)S(1)}, f16[8,8,3584]{2,1,0:T(8,128)(2,1)S(1)}) fusion(f32[4,8,2,8,4096]{4,3,2,1,0:T(8,128)} %bitcast.135, s32[]{:T(128)S(6)} %select_n.77, s32[]{:T(128)S(6)} %select_n.73, s32[]{:T(128)S(6)} %select_n.75, s32[]{:T(128)S(6)} %select_n.71), kind=kLoop, calls=%fused_computation.31 | loop fusion | flops 1376256 | bytes 4128784 | tf_op jit(solution)/shard_map/convert_element_type | solution.py:67
  2.7 3.3 %collective-permute-start = (f16[8,8,3584]{2,1,0:T(8,128)(2,1)S(1)}, f16[8,8,3584]{2,1,0:T(8,128)(2,1)S(1)}, u32[]{:S(2)}, u32[]{:S(2)}) collective-permute-start(f16[8,8,3584]{2,1,0:T(8,128)(2,1)S(1)} %get-tuple-element.26), channel_id=1, source_target_pairs={{0,1},{1,0},{2,3},{3,2},{4,5},{5,4},{6,7},{7,6},{8,9},{9,8},{10,11... | collective-permute-start | bytes 1376264 | tf_op jit(solution)/shard_map/ppermute | solution.py:28
  6.5 1.8 %fusion.20 = f16[4,8,8,512]{3,2,1,0:T(8,128)(2,1)} fusion(f32[4,8,2,8,4096]{4,3,2,1,0:T(8,128)} %bitcast.136, s32[]{:T(128)S(6)} %select_n.73), kind=kLoop, calls=%fused_computation.33 | loop fusion | flops 262144 | bytes 786436 | tf_op jit(solution)/shard_map/convert_element_type | solution.py:74
  8.7 2.1 %fusion.3 = (f16[8,8,3584]{2,1,0:T(8,128)(2,1)S(1)}, f16[8,8,3584]{2,1,0:T(8,128)(2,1)S(1)}, f16[8,8,3584]{2,1,0:T(8,128)(2,1)S(1)}) fusion(f16[8,8,3584]{2,1,0:T(8,128)(2,1)S(1)} %collective-permute-done.2, f32[4,8,2,8,4096]{4,3,2,1,0:T(8,128)} %bitcast.137, s32[]{:T(128)S(6)} %select_n.77, s32[]{:T(128)S(6)} %select_n.72, ...), kind=kLoop, calls=%fused_computation.5 | loop fusion | flops 2752512 | bytes 5505040 | tf_op jit(solution)/shard_map/convert_element_type | solution.py:78
  15.1 2.4 %collective-permute-start.7 = (f16[8,8,3584]{2,1,0:T(8,128)(2,1)S(1)}, f16[8,8,3584]{2,1,0:T(8,128)(2,1)}, u32[]{:S(2)}, u32[]{:S(2)}) collective-permute-start(f16[8,8,3584]{2,1,0:T(8,128)(2,1)S(1)} %get-tuple-element.21), channel_id=1, source_target_pairs={{0,48},{16,0},{32,16},{48,32},{1,49},{17,1},{33,17},{49,33},{2,50}... | collective-permute-start | bytes 1376264 | tf_op jit(solution)/shard_map/ppermute | solution.py:33
  18.2 8.2 %all-to-all-start.1 = ((f16[8,4,8,512]{3,2,1,0:T(8,128)(2,1)}), f16[8,4,8,512]{3,2,1,0:T(8,128)(2,1)S(1)}, u32[]{:S(2)}, u32[]{:S(2)}) async-start(f16[8,4,8,512]{3,2,1,0:T(8,128)(2,1)} %copy.54), calls=%async_computation.1 | async-start | bytes 524288 | tf_op jit(solution)/shard_map/all_to_all | solution.py:37
  27.8 9.8 %collective-permute-done.6 = f16[8,8,3584]{2,1,0:T(8,128)(2,1)} collective-permute-done((f16[8,8,3584]{2,1,0:T(8,128)(2,1)S(1)}, f16[8,8,3584]{2,1,0:T(8,128)(2,1)}, u32[]{:S(2)}, u32[]{:S(2)}) %collective-permute-start.6) | collective-permute-done | bytes 458784 | tf_op jit(solution)/shard_map/ppermute | solution.py:33
  37.6 2.2 %add_convert_fusion = f16[8,8,3584]{2,1,0:T(8,128)(2,1)} fusion(f16[8,8,3584]{2,1,0:T(8,128)(2,1)} %collective-permute-done.7, f16[8,8,3584]{2,1,0:T(8,128)(2,1)} %collective-permute-done.6, f32[8,8,3584]{2,1,0:T(8,128)S(1)} %bitcast_add_fusion, f16[8,8,3584]{2,1,0:T(8,128)(2,1)S(1)} %collective-permute-done.5), kind=kLoop, calls=%fused_computation.22 | loop fusion | flops 1605632 | bytes 2752512 | tf_op jit(solution)/shard_map/convert_element_type | solution.py:94
  39.8 6.5 %all-to-all-start = ((f16[8,8,3584]{2,1,0:T(8,128)(2,1)}), f16[8,8,3584]{2,1,0:T(8,128)(2,1)S(1)}, u32[]{:S(2)}, u32[]{:S(2)}) async-start(f16[8,8,3584]{2,1,0:T(8,128)(2,1)} %add_convert_fusion), calls=%async_computation | async-start | bytes 917504 | tf_op jit(solution)/shard_map/all_to_all | solution.py:37
  46.5 2.5 %collective-permute-start.10 = (f16[8,512]{1,0:T(8,128)(2,1)S(1)}, f16[8,512]{1,0:T(8,128)(2,1)S(1)}, u32[]{:S(2)}, u32[]{:S(2)}) collective-permute-start(f16[8,512]{1,0:T(8,128)(2,1)S(1)} %get-tuple-element.30), channel_id=1, source_target_pairs={{0,48},{16,0},{32,16},{48,32},{1,49},{17,1},{33,17},{49,33},{2,50}... | collective-permute-start | bytes 24584 | tf_op jit(solution)/shard_map/ppermute | solution.py:33
  51.1 1.9 %collective-permute-done.8 = f16[8,512]{1,0:T(8,128)(2,1)S(1)} collective-permute-done((f16[8,512]{1,0:T(8,128)(2,1)S(1)}, f16[8,512]{1,0:T(8,128)(2,1)S(1)}, u32[]{:S(2)}, u32[]{:S(2)}) %collective-permute-start.8) | collective-permute-done | bytes 8224 | tf_op jit(solution)/shard_map/ppermute | solution.py:33
  53.3 9.6 %all-to-all-done = f16[8,8,3584]{2,1,0:T(8,128)(2,1)S(1)} async-done(((f16[8,8,3584]{2,1,0:T(8,128)(2,1)}), f16[8,8,3584]{2,1,0:T(8,128)(2,1)S(1)}, u32[]{:S(2)}, u32[]{:S(2)}) %all-to-all-start) | async-done | bytes 458784 | tf_op jit(solution)/shard_map/all_to_all | solution.py:37
  64.0 7.7 %all-to-all-start.2 = ((f32[256,1,9]{2,1,0:T(1,128)}), f32[256,1,9]{2,1,0:T(1,128)S(1)}, u32[]{:S(2)}, u32[]{:S(2)}) async-start(f32[256,1,9]{2,1,0:T(1,128)} %broadcast_in_dim.4), calls=%async_computation.2 | async-start | bytes 262144 | tf_op jit(solution)/shard_map/all_to_all | solution.py:37
  71.8 12.7 %all-to-all-done.2.reports = f32[256,1,9]{2,1,0:T(1,128)S(1)} async-done(((f32[256,1,9]{2,1,0:T(1,128)}), f32[256,1,9]{2,1,0:T(1,128)S(1)}, u32[]{:S(2)}, u32[]{:S(2)}) %all-to-all-start.2) | async-done | bytes 9248 | tf_op jit(solution)/shard_map/all_to_all | solution.py:37
  84.5 1.7 %shard_map.118 = (bf16[8,8,3328]{2,1,0:T(8,128)(2,1)}, bf16[8,768]{1,0:T(8,128)(2,1)S(1)}, f32[4,9]{1,0:T(4,128)S(1)}) custom-call(s32[1]{0:T(128)} %bitcast.5.section, f32[2]{0:T(128)S(1)} %pad_maximum_fusion.1.fixes, f32[256,1,9]{2,1,0:T(1,128)S(1)} %all-to-all-done.2.reports, f32[8,4096]{1,0:T(8,128)S(1)} %get-tuple-element.27.summed, ...), custom_call_target="tpu_custom_call" | custom-call | tf_op jit(solution)/shard_map/pallas_call | solution.py:142
  86.2 3.5 %all-to-all-start.3 = ((bf16[8,8,3328]{2,1,0:T(8,128)(2,1)}), bf16[8,8,3328]{2,1,0:T(8,128)(2,1)S(1)}, u32[]{:S(2)}, u32[]{:S(2)}) async-start(bf16[8,8,3328]{2,1,0:T(8,128)(2,1)} %get-tuple-element.15), calls=%async_computation.3 | async-start | bytes 851968 | tf_op jit(solution)/shard_map/all_to_all | solution.py:37
  90.8 2.2 %collective-permute-start.17 = (bf16[8,768]{1,0:T(8,128)(2,1)S(1)}, bf16[8,768]{1,0:T(8,128)(2,1)S(1)}, u32[]{:S(2)}, u32[]{:S(2)}) collective-permute-start(bf16[8,768]{1,0:T(8,128)(2,1)S(1)} %get-tuple-element.16), channel_id=1, source_target_pairs={{0,48},{16,0},{32,16},{48,32},{1,49},{17,1},{33,17},{49,33},{2,50}... | collective-permute-start | bytes 36872 | tf_op jit(solution)/shard_map/ppermute | solution.py:33
  94.2 11.2 %all-to-all-done.3.refs_1_ = bf16[8,8,3328]{2,1,0:T(8,128)(2,1)S(1)} async-done(((bf16[8,8,3328]{2,1,0:T(8,128)(2,1)}), bf16[8,8,3328]{2,1,0:T(8,128)(2,1)S(1)}, u32[]{:S(2)}, u32[]{:S(2)}) %all-to-all-start.3) | async-done | bytes 426016 | tf_op jit(solution)/shard_map/all_to_all | solution.py:37
  106.2 3.5 %all-to-all-start.4 = ((bf16[8,4,8,768]{3,2,1,0:T(8,128)(2,1)}), bf16[8,4,8,768]{3,2,1,0:T(8,128)(2,1)S(1)}, u32[]{:S(2)}, u32[]{:S(2)}) async-start(bf16[8,4,8,768]{3,2,1,0:T(8,128)(2,1)} %broadcast_in_dim.5), calls=%async_computation.4 | async-start | bytes 786432 | tf_op jit(solution)/shard_map/all_to_all | solution.py:37
  110.4 2.7 %collective-permute-start.13 = (bf16[8,8,3328]{2,1,0:T(8,128)(2,1)S(1)}, bf16[8,8,3328]{2,1,0:T(8,128)(2,1)S(1)}, u32[]{:S(2)}, u32[]{:S(2)}) collective-permute-start(bf16[8,8,3328]{2,1,0:T(8,128)(2,1)S(1)} %all-to-all-done.3.refs_1_), channel_id=1, source_target_pairs={{0,48},{16,0},{32,16},{48,32},{1,49},{17,1},{33,17},{49,33},{2,50}... | collective-permute-start | bytes 1277960 | tf_op jit(solution)/shard_map/ppermute | solution.py:33
  115.2 9.5 %all-to-all-done.4.refs_3_ = bf16[8,4,8,768]{3,2,1,0:T(8,128)(2,1)S(1)} async-done(((bf16[8,4,8,768]{3,2,1,0:T(8,128)(2,1)}), bf16[8,4,8,768]{3,2,1,0:T(8,128)(2,1)S(1)}, u32[]{:S(2)}, u32[]{:S(2)}) %all-to-all-start.4) | async-done | bytes 393248 | tf_op jit(solution)/shard_map/all_to_all | solution.py:37
  125.7 6.4 %collective-permute-done.11.refs_1_ = bf16[8,8,3328]{2,1,0:T(8,128)(2,1)S(1)} collective-permute-done((bf16[8,8,3328]{2,1,0:T(8,128)(2,1)S(1)}, bf16[8,8,3328]{2,1,0:T(8,128)(2,1)S(1)}, u32[]{:S(2)}, u32[]{:S(2)}) %collective-permute-start.11) | collective-permute-done | bytes 426016 | tf_op jit(solution)/shard_map/ppermute | solution.py:33
  134.0 1.8 %shard_map.119.refs_4_ = bf16[4,8,2,8,4096]{4,3,2,1,0:T(8,128)(2,1)} custom-call(s32[8]{0:T(128)S(1)} %stack.87.refs_0_, bf16[8,8,3328]{2,1,0:T(8,128)(2,1)S(1)} %all-to-all-done.3.refs_1_, bf16[8,8,3328]{2,1,0:T(8,128)(2,1)S(1)} %collective-permute-done.19.refs_2_, bf16[8,8,3328]{2,1,0:T(8,128)(2,1)S(1)} %collective-permute-done.20.refs_3_, ...), custom_call_target="tpu_custom_call" | custom-call | tf_op jit(solution)/shard_map/pallas_call | solution.py:179
  135.8 1.6 %shard_map.120.refs_4_ = bf16[4,8,2,8,4096]{4,3,2,1,0:T(8,128)(2,1)} custom-call(s32[12]{0:T(128)S(1)} %stack.86.refs_0_, bf16[8,8,3328]{2,1,0:T(8,128)(2,1)S(1)} %collective-permute-done.11.refs_1_, bf16[8,8,3328]{2,1,0:T(8,128)(2,1)S(1)} %collective-permute-done.13.refs_2_, ...), custom_call_target="tpu_custom_call", output_to_operand_aliasing={{}: (4, {})} | custom-call | tf_op jit(solution)/shard_map/pallas_call | solution.py:179
  (69 shorter events, 18.7 us)
Async XLA Ops:
  2.7 5.7 %collective-permute-start = (f16[8,8,3584]{2,1,0:T(8,128)(2,1)S(1)}, f16[8,8,3584]{2,1,0:T(8,128)(2,1)S(1)}, u32[]{:S(2)}, u32[]{:S(2)}) collective-permute-start(f16[8,8,3584]{2,1,0:T(8,128)(2,1)S(1)} %get-tuple-element.26), channel_id=1, source_target_pairs={{0,1},{1,0},{2,3},{3,2},{4,5},{5,4},{6,7},{7,6},{8,9},{9,8},{10,11... | collective-permute-start | bytes 1376264 | tf_op jit(solution)/shard_map/ppermute | solution.py:28
  13.3 13.1 %collective-permute-start.4 = (f16[8,8,3584]{2,1,0:T(8,128)(2,1)S(1)}, f16[8,8,3584]{2,1,0:T(8,128)(2,1)}, u32[]{:S(2)}, u32[]{:S(2)}) collective-permute-start(f16[8,8,3584]{2,1,0:T(8,128)(2,1)S(1)} %fusion.15), channel_id=1, source_target_pairs={{0,1},{1,0},{2,3},{3,2},{4,5},{5,4},{6,7},{7,6},{8,9},{9,8},{10,11... | collective-permute-start | bytes 1376264 | tf_op jit(solution)/shard_map/ppermute | solution.py:28
  13.7 14.1 %collective-permute-start.5 = (f16[8,8,3584]{2,1,0:T(8,128)(2,1)S(1)}, f16[8,8,3584]{2,1,0:T(8,128)(2,1)S(1)}, u32[]{:S(2)}, u32[]{:S(2)}) collective-permute-start(f16[8,8,3584]{2,1,0:T(8,128)(2,1)S(1)} %get-tuple-element.23), channel_id=1, source_target_pairs={{0,32},{16,48},{32,0},{48,16},{1,33},{17,49},{33,1},{49,17},{2,34}... | collective-permute-start | bytes 1376264 | tf_op jit(solution)/shard_map/ppermute | solution.py:33
  14.8 22.9 %collective-permute-start.6 = (f16[8,8,3584]{2,1,0:T(8,128)(2,1)S(1)}, f16[8,8,3584]{2,1,0:T(8,128)(2,1)}, u32[]{:S(2)}, u32[]{:S(2)}) collective-permute-start(f16[8,8,3584]{2,1,0:T(8,128)(2,1)S(1)} %get-tuple-element.22), channel_id=1, source_target_pairs={{0,16},{16,32},{32,48},{48,0},{1,17},{17,33},{33,49},{49,1},{2,18}... | collective-permute-start | bytes 1376264 | tf_op jit(solution)/shard_map/ppermute | solution.py:33
  15.1 22.6 %collective-permute-start.7 = (f16[8,8,3584]{2,1,0:T(8,128)(2,1)S(1)}, f16[8,8,3584]{2,1,0:T(8,128)(2,1)}, u32[]{:S(2)}, u32[]{:S(2)}) collective-permute-start(f16[8,8,3584]{2,1,0:T(8,128)(2,1)S(1)} %get-tuple-element.21), channel_id=1, source_target_pairs={{0,48},{16,0},{32,16},{48,32},{1,49},{17,1},{33,17},{49,33},{2,50}... | collective-permute-start | bytes 1376264 | tf_op jit(solution)/shard_map/ppermute | solution.py:33
  18.2 21.6 %all-to-all-start.1 = ((f16[8,4,8,512]{3,2,1,0:T(8,128)(2,1)}), f16[8,4,8,512]{3,2,1,0:T(8,128)(2,1)S(1)}, u32[]{:S(2)}, u32[]{:S(2)}) async-start(f16[8,4,8,512]{3,2,1,0:T(8,128)(2,1)} %copy.54), calls=%async_computation.1 | async-start | bytes 524288 | tf_op jit(solution)/shard_map/all_to_all | solution.py:37
  39.8 23.0 %all-to-all-start = ((f16[8,8,3584]{2,1,0:T(8,128)(2,1)}), f16[8,8,3584]{2,1,0:T(8,128)(2,1)S(1)}, u32[]{:S(2)}, u32[]{:S(2)}) async-start(f16[8,8,3584]{2,1,0:T(8,128)(2,1)} %add_convert_fusion), calls=%async_computation | async-start | bytes 917504 | tf_op jit(solution)/shard_map/all_to_all | solution.py:37
  46.5 4.6 %collective-permute-start.10 = (f16[8,512]{1,0:T(8,128)(2,1)S(1)}, f16[8,512]{1,0:T(8,128)(2,1)S(1)}, u32[]{:S(2)}, u32[]{:S(2)}) collective-permute-start(f16[8,512]{1,0:T(8,128)(2,1)S(1)} %get-tuple-element.30), channel_id=1, source_target_pairs={{0,48},{16,0},{32,16},{48,32},{1,49},{17,1},{33,17},{49,33},{2,50}... | collective-permute-start | bytes 24584 | tf_op jit(solution)/shard_map/ppermute | solution.py:33
  49.0 4.0 %collective-permute-start.8 = (f16[8,512]{1,0:T(8,128)(2,1)S(1)}, f16[8,512]{1,0:T(8,128)(2,1)S(1)}, u32[]{:S(2)}, u32[]{:S(2)}) collective-permute-start(f16[8,512]{1,0:T(8,128)(2,1)S(1)} %get-tuple-element.29), channel_id=1, source_target_pairs={{0,32},{16,48},{32,0},{48,16},{1,33},{17,49},{33,1},{49,17},{2,34}... | collective-permute-start | bytes 24584 | tf_op jit(solution)/shard_map/ppermute | solution.py:33
  49.5 3.7 %collective-permute-start.9 = (f16[8,512]{1,0:T(8,128)(2,1)S(1)}, f16[8,512]{1,0:T(8,128)(2,1)S(1)}, u32[]{:S(2)}, u32[]{:S(2)}) collective-permute-start(f16[8,512]{1,0:T(8,128)(2,1)S(1)} %get-tuple-element.31), channel_id=1, source_target_pairs={{0,16},{16,32},{32,48},{48,0},{1,17},{17,33},{33,49},{49,1},{2,18}... | collective-permute-start | bytes 24584 | tf_op jit(solution)/shard_map/ppermute | solution.py:33
  64.0 20.6 %all-to-all-start.2 = ((f32[256,1,9]{2,1,0:T(1,128)}), f32[256,1,9]{2,1,0:T(1,128)S(1)}, u32[]{:S(2)}, u32[]{:S(2)}) async-start(f32[256,1,9]{2,1,0:T(1,128)} %broadcast_in_dim.4), calls=%async_computation.2 | async-start | bytes 262144 | tf_op jit(solution)/shard_map/all_to_all | solution.py:37
  86.2 19.2 %all-to-all-start.3 = ((bf16[8,8,3328]{2,1,0:T(8,128)(2,1)}), bf16[8,8,3328]{2,1,0:T(8,128)(2,1)S(1)}, u32[]{:S(2)}, u32[]{:S(2)}) async-start(bf16[8,8,3328]{2,1,0:T(8,128)(2,1)} %get-tuple-element.15), calls=%async_computation.3 | async-start | bytes 851968 | tf_op jit(solution)/shard_map/all_to_all | solution.py:37
  89.7 4.1 %collective-permute-start.15 = (bf16[8,768]{1,0:T(8,128)(2,1)S(1)}, bf16[8,768]{1,0:T(8,128)(2,1)S(1)}, u32[]{:S(2)}, u32[]{:S(2)}) collective-permute-start(bf16[8,768]{1,0:T(8,128)(2,1)S(1)} %get-tuple-element.16), channel_id=1, source_target_pairs={{0,32},{16,48},{32,0},{48,16},{1,33},{17,49},{33,1},{49,17},{2,34}... | collective-permute-start | bytes 36872 | tf_op jit(solution)/shard_map/ppermute | solution.py:33
  90.4 3.8 %collective-permute-start.16 = (bf16[8,768]{1,0:T(8,128)(2,1)S(1)}, bf16[8,768]{1,0:T(8,128)(2,1)S(1)}, u32[]{:S(2)}, u32[]{:S(2)}) collective-permute-start(bf16[8,768]{1,0:T(8,128)(2,1)S(1)} %get-tuple-element.16), channel_id=1, source_target_pairs={{0,16},{16,32},{32,48},{48,0},{1,17},{17,33},{33,49},{49,1},{2,18}... | collective-permute-start | bytes 36872 | tf_op jit(solution)/shard_map/ppermute | solution.py:33
  90.8 3.3 %collective-permute-start.17 = (bf16[8,768]{1,0:T(8,128)(2,1)S(1)}, bf16[8,768]{1,0:T(8,128)(2,1)S(1)}, u32[]{:S(2)}, u32[]{:S(2)}) collective-permute-start(bf16[8,768]{1,0:T(8,128)(2,1)S(1)} %get-tuple-element.16), channel_id=1, source_target_pairs={{0,48},{16,0},{32,16},{48,32},{1,49},{17,1},{33,17},{49,33},{2,50}... | collective-permute-start | bytes 36872 | tf_op jit(solution)/shard_map/ppermute | solution.py:33
  106.2 18.5 %all-to-all-start.4 = ((bf16[8,4,8,768]{3,2,1,0:T(8,128)(2,1)}), bf16[8,4,8,768]{3,2,1,0:T(8,128)(2,1)S(1)}, u32[]{:S(2)}, u32[]{:S(2)}) async-start(bf16[8,4,8,768]{3,2,1,0:T(8,128)(2,1)} %broadcast_in_dim.5), calls=%async_computation.4 | async-start | bytes 786432 | tf_op jit(solution)/shard_map/all_to_all | solution.py:37
  109.6 15.6 %collective-permute-start.20 = (bf16[8,8,3328]{2,1,0:T(8,128)(2,1)S(1)}, bf16[8,8,3328]{2,1,0:T(8,128)(2,1)S(1)}, u32[]{:S(2)}, u32[]{:S(2)}) collective-permute-start(bf16[8,8,3328]{2,1,0:T(8,128)(2,1)S(1)} %all-to-all-done.3.refs_1_), channel_id=1, source_target_pairs={{0,32},{16,48},{32,0},{48,16},{1,33},{17,49},{33,1},{49,17},{2,34}... | collective-permute-start | bytes 1277960 | tf_op jit(solution)/shard_map/ppermute | solution.py:33
  110.4 21.7 %collective-permute-start.11 = (bf16[8,8,3328]{2,1,0:T(8,128)(2,1)S(1)}, bf16[8,8,3328]{2,1,0:T(8,128)(2,1)S(1)}, u32[]{:S(2)}, u32[]{:S(2)}) collective-permute-start(bf16[8,8,3328]{2,1,0:T(8,128)(2,1)S(1)} %all-to-all-done.3.refs_1_), channel_id=1, source_target_pairs={{0,16},{16,32},{32,48},{48,0},{1,17},{17,33},{33,49},{49,1},{2,18}... | collective-permute-start | bytes 1277960 | tf_op jit(solution)/shard_map/ppermute | solution.py:33
  110.4 22.2 %collective-permute-start.13 = (bf16[8,8,3328]{2,1,0:T(8,128)(2,1)S(1)}, bf16[8,8,3328]{2,1,0:T(8,128)(2,1)S(1)}, u32[]{:S(2)}, u32[]{:S(2)}) collective-permute-start(bf16[8,8,3328]{2,1,0:T(8,128)(2,1)S(1)} %all-to-all-done.3.refs_1_), channel_id=1, source_target_pairs={{0,48},{16,0},{32,16},{48,32},{1,49},{17,1},{33,17},{49,33},{2,50}... | collective-permute-start | bytes 1277960 | tf_op jit(solution)/shard_map/ppermute | solution.py:33
  124.7 12.7 %collective-permute-start.18 = (bf16[8,4,8,768]{3,2,1,0:T(8,128)(2,1)S(1)}, bf16[8,4,8,768]{3,2,1,0:T(8,128)(2,1)S(1)}, u32[]{:S(2)}, u32[]{:S(2)}) collective-permute-start(bf16[8,4,8,768]{3,2,1,0:T(8,128)(2,1)S(1)} %all-to-all-done.4.refs_3_), channel_id=1, source_target_pairs={{0,1},{1,0},{2,3},{3,2},{4,5},{5,4},{6,7},{7,6},{8,9},{9,8},{10,11... | collective-permute-start | bytes 1179656 | tf_op jit(solution)/shard_map/ppermute | solution.py:28
  125.2 8.8 %collective-permute-start.19 = (bf16[8,8,3328]{2,1,0:T(8,128)(2,1)S(1)}, bf16[8,8,3328]{2,1,0:T(8,128)(2,1)S(1)}, u32[]{:S(2)}, u32[]{:S(2)}) collective-permute-start(bf16[8,8,3328]{2,1,0:T(8,128)(2,1)S(1)} %all-to-all-done.3.refs_1_), channel_id=1, source_target_pairs={{0,1},{1,0},{2,3},{3,2},{4,5},{5,4},{6,7},{7,6},{8,9},{9,8},{10,11... | collective-permute-start | bytes 1277960 | tf_op jit(solution)/shard_map/ppermute | solution.py:28
  125.2 8.8 %collective-permute-start.21 = (bf16[8,8,3328]{2,1,0:T(8,128)(2,1)S(1)}, bf16[8,8,3328]{2,1,0:T(8,128)(2,1)S(1)}, u32[]{:S(2)}, u32[]{:S(2)}) collective-permute-start(bf16[8,8,3328]{2,1,0:T(8,128)(2,1)S(1)} %collective-permute-done.20.refs_3_), channel_id=1, source_target_pairs={{0,1},{1,0},{2,3},{3,2},{4,5},{5,4},{6,7},{7,6},{8,9},{9,8},{10,11... | collective-permute-start | bytes 1277960 | tf_op jit(solution)/shard_map/ppermute | solution.py:28
  132.1 5.3 %collective-permute-start.12 = (bf16[8,8,3328]{2,1,0:T(8,128)(2,1)S(1)}, bf16[8,8,3328]{2,1,0:T(8,128)(2,1)S(1)}, u32[]{:S(2)}, u32[]{:S(2)}) collective-permute-start(bf16[8,8,3328]{2,1,0:T(8,128)(2,1)S(1)} %collective-permute-done.11.refs_1_), channel_id=1, source_target_pairs={{0,1},{1,0},{2,3},{3,2},{4,5},{5,4},{6,7},{7,6},{8,9},{9,8},{10,11... | collective-permute-start | bytes 1277960 | tf_op jit(solution)/shard_map/ppermute | solution.py:28
  132.6 4.8 %collective-permute-start.14 = (bf16[8,8,3328]{2,1,0:T(8,128)(2,1)S(1)}, bf16[8,8,3328]{2,1,0:T(8,128)(2,1)S(1)}, u32[]{:S(2)}, u32[]{:S(2)}) collective-permute-start(bf16[8,8,3328]{2,1,0:T(8,128)(2,1)S(1)} %collective-permute-done.13.refs_2_), channel_id=1, source_target_pairs={{0,1},{1,0},{2,3},{3,2},{4,5},{5,4},{6,7},{7,6},{8,9},{9,8},{10,11... | collective-permute-start | bytes 1277960 | tf_op jit(solution)/shard_map/ppermute | solution.py:28
  (7 other events, 280.2 us)

commit v4 on v3

--- a/solution.py
+++ b/solution.py
@@ -18,7 +18,7 @@
 epsilon = 1e-08
 
 WIRE = jnp.float16
-SCALE = 0.5
+SCALE = 0.25
 
 SUM_SHARE = 14
 GATHER_SHARE = 13
@@ -69,16 +69,23 @@
     def summed_chip(source, k, other):
         return piece(source, (x + k) % n_x, core, 0, wide)[0] + other.astype(jnp.float32)
 
-    order = hops(n_x)
-    sent = [encoded(parts, k) for k in order]
-    sent_b = piece(after(parts, *sent), None, 1 - core, wide, width - wide).astype(WIRE)
-    other = [swapped(v) for v in sent]
+    far, *near = hops(n_x)
+    far_sent = encoded(parts, far)
+    near_sent = [encoded(after(parts, far_sent), k) for k in near]
+    far_other = swapped(far_sent)
+    near_other = [swapped(v) for v in near_sent]
+    far_chip = summed_chip(parts, far, far_other).astype(WIRE)
+    far_in = shifted(far_chip, "x", far)
+    late = after(parts, far_chip)
+    chips = [
+        summed_chip(late, k, v).astype(WIRE)
+        for k, v in zip(near, near_other, strict=True)
+    ]
+    near_in = [shifted(v, "x", k) for k, v in zip(near, chips, strict=True)]
+    late = after(parts, *chips)
+    sent_b = piece(late, None, 1 - core, wide, width - wide).astype(WIRE)
     other_b = swapped(sent_b)
-    chips = [
-        summed_chip(parts, k, v).astype(WIRE) for k, v in zip(order, other, strict=True)
-    ]
-    arrived = [shifted(v, "x", k) for k, v in zip(order, chips, strict=True)]
-    late = after(parts, *chips)
+    late = after(parts, sent_b)
     chip_b = piece(late, None, core, wide, width - wide)
     chip_b = chip_b + other_b.astype(jnp.float32)
     chip_b = chip_b.transpose(1, 0, 2, 3).astype(WIRE)
@@ -87,8 +94,9 @@
     late = after(parts, chip_b)
     own = encoded(late, 0)
     own = swapped(own)
-    a_x = lax.optimization_barrier(summed_chip(late, 0, own))
-    for value in arrived:
+    a_x = summed_chip(late, 0, own) + far_in.astype(jnp.float32)
+    a_x = lax.optimization_barrier(a_x)
+    for value in near_in:
         a_x = a_x + value.astype(jnp.float32)
     b_sent = [shifted(at(b_z, (x + k) % n_x).astype(WIRE), "x", k) for k in hops(n_x)]
     a_z = exchanged(a_x.astype(WIRE), "z").astype(jnp.float32).sum(axis=0)

time: 140 us -> 139 us (level)
  waiting for transfers between devices: 62.9 us -> 60.5 us
    ppermute x12, waiting for transfers between devices: 19.4 us -> 15.9 us  [shifted(): return lax.ppermute(value, axis, [(i, (i + k) % n) for i in range(n)])]
    convert_element_type x2 -> x3, other arithmetic: 3.23 us -> 4.13 us  [encoded(): return piece(source, (x + k) % n_x, 1 - core, 0, wide)[0].astype(WIRE)]
    convert_element_type x2 -> x3, other arithmetic: 3.93 us -> 4.33 us  [the longest x1 1.86 us: reduced_rows(): summed_chip(late, k, v).astype(WIRE)]
  transfers between devices with their start and end apart: 27 -> 27, of which waited for: 11 -> 13; matrix products, arithmetic and copies ran while one was open for 8% -> 9% of each run, Pallas kernels for 2% -> 2%
where the time goes in v4:
time: 139 us; the launch traced here: 138 us
  waiting for transfers between devices  60.5 us (44%)
  starting transfers between devices  49.4 us (36%)
  other arithmetic  15 us (11%)
  Pallas kernels  6.67 us (5%)
  between operations  3.69 us (3%)
  local copies, waits for them, and re-layouts  3.13 us (2%)
    all_to_all x5, waiting for transfers between devices, exchanged(): return lax.all_to_all(value, axis, 0, 0, tiled=True)  43.4 us
    all_to_all x5, starting transfers between devices, exchanged(): return lax.all_to_all(value, axis, 0, 0, tiled=True)  29.3 us
    ppermute x12, waiting for transfers between devices, shifted(): return lax.ppermute(value, axis, [(i, (i + k) % n) for i in range(n)])  15.9 us
    ppermute x12, starting transfers between devices, shifted(): return lax.ppermute(value, axis, [(i, (i + k) % n) for i in range(n)])  14.2 us
    ppermute x10, starting transfers between devices, swapped(): return lax.ppermute(value, 'c', [(0, 1), (1, 0)])  6 us
    pallas_call x3, Pallas kernels, placed_rows(): pl.pallas_call(kernel, out_shape=jax.ShapeDtypeStruct(shape, pieces[0][0]...  5 us
    convert_element_type x3, other arithmetic, encoded(): return piece(source, (x + k) % n_x, 1 - core, 0, wide)[0].astype(WIRE)  4.13 us
  transfers between devices with their start and end apart: 27, of which 13 were waited for; matrix products, arithmetic and copies ran while one was open for 9% of the time, Pallas kernels for 2%

profile of v4, /device:TPU:1, one launch (start us, length us, event | category | flops | bytes accessed | tf_op | source)
XLA Modules:
  0.0 138.3 jit_solution(13306283583507024511)
XLA Ops:
  1.9 3.3 %collective-permute-start = (f16[8,8,3584]{2,1,0:T(8,128)(2,1)S(1)}, f16[8,8,3584]{2,1,0:T(8,128)(2,1)S(1)}, u32[]{:S(2)}, u32[]{:S(2)}) collective-permute-start(f16[8,8,3584]{2,1,0:T(8,128)(2,1)S(1)} %fusion.12), channel_id=1, source_target_pairs={{0,1},{1,0},{2,3},{3,2},{4,5},{5,4},{6,7},{7,6},{8,9},{9,8},{10,11... | collective-permute-start | bytes 1376264 | tf_op jit(solution)/shard_map/ppermute | solution.py:28
  5.2 1.6 %fusion.10 = (f16[8,8,3584]{2,1,0:T(8,128)(2,1)S(1)}, f16[8,8,3584]{2,1,0:T(8,128)(2,1)S(1)}) fusion(s32[]{:T(128)S(6)} %select_n.77, s32[]{:T(128)S(6)} %select_n.73, s32[]{:T(128)S(6)} %select_n.75, f32[4,8,2,8,4096]{4,3,2,1,0:T(8,128)} %bitcast.106), kind=kLoop, calls=%fused_computation.24 | loop fusion | flops 917504 | bytes 2752524 | tf_op jit(solution)/shard_map/convert_element_type | solution.py:67
  9.5 1.9 %fusion.6 = (f16[8,8,3584]{2,1,0:T(8,128)(2,1)S(1)}, f16[8,8,3584]{2,1,0:T(8,128)(2,1)S(1)}) fusion(f16[8,8,3584]{2,1,0:T(8,128)(2,1)} %collective-permute-done.2, s32[]{:T(128)S(6)} %select_n.77, s32[]{:T(128)S(6)} %select_n.72, f16[8,8,3584]{2,1,0:T(8,128)(2,1)S(1)} %collective-permute-done.1, s32[]{:T(128)S(6)} %select_n.75, ...), kind=kLoop, calls=%fused_computation.11 | loop fusion | flops 1835008 | bytes 3670028 | tf_op jit(solution)/shard_map/convert_element_type | solution.py:81
  17.2 2.4 %collective-permute-start.7 = (f16[8,8,3584]{2,1,0:T(8,128)(2,1)S(1)}, f16[8,8,3584]{2,1,0:T(8,128)(2,1)}, u32[]{:S(2)}, u32[]{:S(2)}) collective-permute-start(f16[8,8,3584]{2,1,0:T(8,128)(2,1)S(1)} %get-tuple-element.25), channel_id=1, source_target_pairs={{0,48},{16,0},{32,16},{48,32},{1,49},{17,1},{33,17},{49,33},{2,50}... | collective-permute-start | bytes 1376264 | tf_op jit(solution)/shard_map/ppermute | solution.py:33
  20.3 8.2 %all-to-all-start.1 = ((f16[8,4,8,512]{3,2,1,0:T(8,128)(2,1)}), f16[8,4,8,512]{3,2,1,0:T(8,128)(2,1)S(1)}, u32[]{:S(2)}, u32[]{:S(2)}) async-start(f16[8,4,8,512]{3,2,1,0:T(8,128)(2,1)} %copy.54), calls=%async_computation.1 | async-start | bytes 524288 | tf_op jit(solution)/shard_map/all_to_all | solution.py:37
  29.9 6.8 %collective-permute-done.6 = f16[8,8,3584]{2,1,0:T(8,128)(2,1)} collective-permute-done((f16[8,8,3584]{2,1,0:T(8,128)(2,1)S(1)}, f16[8,8,3584]{2,1,0:T(8,128)(2,1)}, u32[]{:S(2)}, u32[]{:S(2)}) %collective-permute-start.6) | collective-permute-done | bytes 458784 | tf_op jit(solution)/shard_map/ppermute | solution.py:33
  36.6 2.1 %add_convert_fusion = f16[8,8,3584]{2,1,0:T(8,128)(2,1)} fusion(f16[8,8,3584]{2,1,0:T(8,128)(2,1)} %collective-permute-done.7, f32[8,8,3584]{2,1,0:T(8,128)S(1)} %fusion.5, f16[8,8,3584]{2,1,0:T(8,128)(2,1)} %collective-permute-done.6), kind=kLoop, calls=%fused_computation.15 | loop fusion | flops 1146880 | bytes 2293760 | tf_op jit(solution)/shard_map/convert_element_type | solution.py:102
  39.0 6.2 %all-to-all-start = ((f16[8,8,3584]{2,1,0:T(8,128)(2,1)}), f16[8,8,3584]{2,1,0:T(8,128)(2,1)S(1)}, u32[]{:S(2)}, u32[]{:S(2)}) async-start(f16[8,8,3584]{2,1,0:T(8,128)(2,1)} %add_convert_fusion), calls=%async_computation | async-start | bytes 917504 | tf_op jit(solution)/shard_map/all_to_all | solution.py:37
  45.4 2.5 %collective-permute-start.10 = (f16[8,512]{1,0:T(8,128)(2,1)S(1)}, f16[8,512]{1,0:T(8,128)(2,1)S(1)}, u32[]{:S(2)}, u32[]{:S(2)}) collective-permute-start(f16[8,512]{1,0:T(8,128)(2,1)S(1)} %get-tuple-element.32), channel_id=1, source_target_pairs={{0,48},{16,0},{32,16},{48,32},{1,49},{17,1},{33,17},{49,33},{2,50}... | collective-permute-start | bytes 24584 | tf_op jit(solution)/shard_map/ppermute | solution.py:33
  50.4 1.5 %collective-permute-done.8 = f16[8,512]{1,0:T(8,128)(2,1)S(1)} collective-permute-done((f16[8,512]{1,0:T(8,128)(2,1)S(1)}, f16[8,512]{1,0:T(8,128)(2,1)S(1)}, u32[]{:S(2)}, u32[]{:S(2)}) %collective-permute-start.8) | collective-permute-done | bytes 8224 | tf_op jit(solution)/shard_map/ppermute | solution.py:33
  52.1 9.7 %all-to-all-done = f16[8,8,3584]{2,1,0:T(8,128)(2,1)S(1)} async-done(((f16[8,8,3584]{2,1,0:T(8,128)(2,1)}), f16[8,8,3584]{2,1,0:T(8,128)(2,1)S(1)}, u32[]{:S(2)}, u32[]{:S(2)}) %all-to-all-start) | async-done | bytes 458784 | tf_op jit(solution)/shard_map/all_to_all | solution.py:37
  62.9 8.0 %all-to-all-start.2 = ((f32[256,1,9]{2,1,0:T(1,128)}), f32[256,1,9]{2,1,0:T(1,128)S(1)}, u32[]{:S(2)}, u32[]{:S(2)}) async-start(f32[256,1,9]{2,1,0:T(1,128)} %broadcast_in_dim.4), calls=%async_computation.2 | async-start | bytes 262144 | tf_op jit(solution)/shard_map/all_to_all | solution.py:37
  71.0 12.7 %all-to-all-done.2.reports = f32[256,1,9]{2,1,0:T(1,128)S(1)} async-done(((f32[256,1,9]{2,1,0:T(1,128)}), f32[256,1,9]{2,1,0:T(1,128)S(1)}, u32[]{:S(2)}, u32[]{:S(2)}) %all-to-all-start.2) | async-done | bytes 9248 | tf_op jit(solution)/shard_map/all_to_all | solution.py:37
  83.7 1.7 %shard_map.118 = (bf16[8,8,3328]{2,1,0:T(8,128)(2,1)}, bf16[8,768]{1,0:T(8,128)(2,1)S(1)}, f32[4,9]{1,0:T(4,128)S(1)}) custom-call(s32[1]{0:T(128)} %bitcast.5.section, f32[2]{0:T(128)S(1)} %pad_maximum_fusion.1.fixes, f32[256,1,9]{2,1,0:T(1,128)S(1)} %all-to-all-done.2.reports, f32[8,4096]{1,0:T(8,128)S(1)} %get-tuple-element.29.summed, ...), custom_call_target="tpu_custom_call" | custom-call | tf_op jit(solution)/shard_map/pallas_call | solution.py:150
  85.4 3.5 %all-to-all-start.3 = ((bf16[8,8,3328]{2,1,0:T(8,128)(2,1)}), bf16[8,8,3328]{2,1,0:T(8,128)(2,1)S(1)}, u32[]{:S(2)}, u32[]{:S(2)}) async-start(bf16[8,8,3328]{2,1,0:T(8,128)(2,1)} %get-tuple-element.19), calls=%async_computation.3 | async-start | bytes 851968 | tf_op jit(solution)/shard_map/all_to_all | solution.py:37
  90.0 2.2 %collective-permute-start.17 = (bf16[8,768]{1,0:T(8,128)(2,1)S(1)}, bf16[8,768]{1,0:T(8,128)(2,1)S(1)}, u32[]{:S(2)}, u32[]{:S(2)}) collective-permute-start(bf16[8,768]{1,0:T(8,128)(2,1)S(1)} %get-tuple-element.20), channel_id=1, source_target_pairs={{0,48},{16,0},{32,16},{48,32},{1,49},{17,1},{33,17},{49,33},{2,50}... | collective-permute-start | bytes 36872 | tf_op jit(solution)/shard_map/ppermute | solution.py:33
  93.3 11.2 %all-to-all-done.3.refs_1_ = bf16[8,8,3328]{2,1,0:T(8,128)(2,1)S(1)} async-done(((bf16[8,8,3328]{2,1,0:T(8,128)(2,1)}), bf16[8,8,3328]{2,1,0:T(8,128)(2,1)S(1)}, u32[]{:S(2)}, u32[]{:S(2)}) %all-to-all-start.3) | async-done | bytes 426016 | tf_op jit(solution)/shard_map/all_to_all | solution.py:37
  105.3 3.5 %all-to-all-start.4 = ((bf16[8,4,8,768]{3,2,1,0:T(8,128)(2,1)}), bf16[8,4,8,768]{3,2,1,0:T(8,128)(2,1)S(1)}, u32[]{:S(2)}, u32[]{:S(2)}) async-start(bf16[8,4,8,768]{3,2,1,0:T(8,128)(2,1)} %broadcast_in_dim.5), calls=%async_computation.4 | async-start | bytes 786432 | tf_op jit(solution)/shard_map/all_to_all | solution.py:37
  109.5 2.7 %collective-permute-start.13 = (bf16[8,8,3328]{2,1,0:T(8,128)(2,1)S(1)}, bf16[8,8,3328]{2,1,0:T(8,128)(2,1)S(1)}, u32[]{:S(2)}, u32[]{:S(2)}) collective-permute-start(bf16[8,8,3328]{2,1,0:T(8,128)(2,1)S(1)} %all-to-all-done.3.refs_1_), channel_id=1, source_target_pairs={{0,48},{16,0},{32,16},{48,32},{1,49},{17,1},{33,17},{49,33},{2,50}... | collective-permute-start | bytes 1277960 | tf_op jit(solution)/shard_map/ppermute | solution.py:33
  114.3 9.5 %all-to-all-done.4.refs_3_ = bf16[8,4,8,768]{3,2,1,0:T(8,128)(2,1)S(1)} async-done(((bf16[8,4,8,768]{3,2,1,0:T(8,128)(2,1)}), bf16[8,4,8,768]{3,2,1,0:T(8,128)(2,1)S(1)}, u32[]{:S(2)}, u32[]{:S(2)}) %all-to-all-start.4) | async-done | bytes 393248 | tf_op jit(solution)/shard_map/all_to_all | solution.py:37
  124.8 6.4 %collective-permute-done.11.refs_1_ = bf16[8,8,3328]{2,1,0:T(8,128)(2,1)S(1)} collective-permute-done((bf16[8,8,3328]{2,1,0:T(8,128)(2,1)S(1)}, bf16[8,8,3328]{2,1,0:T(8,128)(2,1)S(1)}, u32[]{:S(2)}, u32[]{:S(2)}) %collective-permute-start.11) | collective-permute-done | bytes 426016 | tf_op jit(solution)/shard_map/ppermute | solution.py:33
  133.1 1.8 %shard_map.119.refs_4_ = bf16[4,8,2,8,4096]{4,3,2,1,0:T(8,128)(2,1)} custom-call(s32[8]{0:T(128)S(1)} %stack.87.refs_0_, bf16[8,8,3328]{2,1,0:T(8,128)(2,1)S(1)} %all-to-all-done.3.refs_1_, bf16[8,8,3328]{2,1,0:T(8,128)(2,1)S(1)} %collective-permute-done.19.refs_2_, bf16[8,8,3328]{2,1,0:T(8,128)(2,1)S(1)} %collective-permute-done.20.refs_3_, ...), custom_call_target="tpu_custom_call" | custom-call | tf_op jit(solution)/shard_map/pallas_call | solution.py:187
  134.9 1.6 %shard_map.120.refs_4_ = bf16[4,8,2,8,4096]{4,3,2,1,0:T(8,128)(2,1)} custom-call(s32[12]{0:T(128)S(1)} %stack.86.refs_0_, bf16[8,8,3328]{2,1,0:T(8,128)(2,1)S(1)} %collective-permute-done.11.refs_1_, bf16[8,8,3328]{2,1,0:T(8,128)(2,1)S(1)} %collective-permute-done.13.refs_2_, ...), custom_call_target="tpu_custom_call", output_to_operand_aliasing={{}: (4, {})} | custom-call | tf_op jit(solution)/shard_map/pallas_call | solution.py:187
  136.6 1.6 %shard_map.121 = bf16[4,8,2,8,4096]{4,3,2,1,0:T(8,128)(2,1)} custom-call(s32[12]{0:T(128)S(1)} %stack.35.refs_0_, bf16[8,8,3328]{2,1,0:T(8,128)(2,1)S(1)} %collective-permute-done.12.refs_1_, bf16[8,8,3328]{2,1,0:T(8,128)(2,1)S(1)} %collective-permute-done.14.refs_2_, ...), custom_call_target="tpu_custom_call", output_to_operand_aliasing={{}: (4, {})} | custom-call | tf_op jit(solution)/shard_map/pallas_call | solution.py:187
  (71 shorter events, 22.3 us)
Async XLA Ops:
  1.9 5.5 %collective-permute-start = (f16[8,8,3584]{2,1,0:T(8,128)(2,1)S(1)}, f16[8,8,3584]{2,1,0:T(8,128)(2,1)S(1)}, u32[]{:S(2)}, u32[]{:S(2)}) collective-permute-start(f16[8,8,3584]{2,1,0:T(8,128)(2,1)S(1)} %fusion.12), channel_id=1, source_target_pairs={{0,1},{1,0},{2,3},{3,2},{4,5},{5,4},{6,7},{7,6},{8,9},{9,8},{10,11... | collective-permute-start | bytes 1376264 | tf_op jit(solution)/shard_map/ppermute | solution.py:28
  12.7 15.8 %collective-permute-start.5 = (f16[8,8,3584]{2,1,0:T(8,128)(2,1)S(1)}, f16[8,8,3584]{2,1,0:T(8,128)(2,1)S(1)}, u32[]{:S(2)}, u32[]{:S(2)}) collective-permute-start(f16[8,8,3584]{2,1,0:T(8,128)(2,1)S(1)} %fusion.3), channel_id=1, source_target_pairs={{0,32},{16,48},{32,0},{48,16},{1,33},{17,49},{33,1},{49,17},{2,34}... | collective-permute-start | bytes 1376264 | tf_op jit(solution)/shard_map/ppermute | solution.py:33
  16.5 12.0 %collective-permute-start.4 = (f16[8,8,3584]{2,1,0:T(8,128)(2,1)S(1)}, f16[8,8,3584]{2,1,0:T(8,128)(2,1)S(1)}, u32[]{:S(2)}, u32[]{:S(2)}) collective-permute-start(f16[8,8,3584]{2,1,0:T(8,128)(2,1)S(1)} %fusion.11), channel_id=1, source_target_pairs={{0,1},{1,0},{2,3},{3,2},{4,5},{5,4},{6,7},{7,6},{8,9},{9,8},{10,11... | collective-permute-start | bytes 1376264 | tf_op jit(solution)/shard_map/ppermute | solution.py:28
  16.9 19.7 %collective-permute-start.6 = (f16[8,8,3584]{2,1,0:T(8,128)(2,1)S(1)}, f16[8,8,3584]{2,1,0:T(8,128)(2,1)}, u32[]{:S(2)}, u32[]{:S(2)}) collective-permute-start(f16[8,8,3584]{2,1,0:T(8,128)(2,1)S(1)} %get-tuple-element.26), channel_id=1, source_target_pairs={{0,16},{16,32},{32,48},{48,0},{1,17},{17,33},{33,49},{49,1},{2,18}... | collective-permute-start | bytes 1376264 | tf_op jit(solution)/shard_map/ppermute | solution.py:33
  17.2 19.4 %collective-permute-start.7 = (f16[8,8,3584]{2,1,0:T(8,128)(2,1)S(1)}, f16[8,8,3584]{2,1,0:T(8,128)(2,1)}, u32[]{:S(2)}, u32[]{:S(2)}) collective-permute-start(f16[8,8,3584]{2,1,0:T(8,128)(2,1)S(1)} %get-tuple-element.25), channel_id=1, source_target_pairs={{0,48},{16,0},{32,16},{48,32},{1,49},{17,1},{33,17},{49,33},{2,50}... | collective-permute-start | bytes 1376264 | tf_op jit(solution)/shard_map/ppermute | solution.py:33
  20.3 18.7 %all-to-all-start.1 = ((f16[8,4,8,512]{3,2,1,0:T(8,128)(2,1)}), f16[8,4,8,512]{3,2,1,0:T(8,128)(2,1)S(1)}, u32[]{:S(2)}, u32[]{:S(2)}) async-start(f16[8,4,8,512]{3,2,1,0:T(8,128)(2,1)} %copy.54), calls=%async_computation.1 | async-start | bytes 524288 | tf_op jit(solution)/shard_map/all_to_all | solution.py:37
  39.0 22.7 %all-to-all-start = ((f16[8,8,3584]{2,1,0:T(8,128)(2,1)}), f16[8,8,3584]{2,1,0:T(8,128)(2,1)S(1)}, u32[]{:S(2)}, u32[]{:S(2)}) async-start(f16[8,8,3584]{2,1,0:T(8,128)(2,1)} %add_convert_fusion), calls=%async_computation | async-start | bytes 917504 | tf_op jit(solution)/shard_map/all_to_all | solution.py:37
  45.4 5.0 %collective-permute-start.10 = (f16[8,512]{1,0:T(8,128)(2,1)S(1)}, f16[8,512]{1,0:T(8,128)(2,1)S(1)}, u32[]{:S(2)}, u32[]{:S(2)}) collective-permute-start(f16[8,512]{1,0:T(8,128)(2,1)S(1)} %get-tuple-element.32), channel_id=1, source_target_pairs={{0,48},{16,0},{32,16},{48,32},{1,49},{17,1},{33,17},{49,33},{2,50}... | collective-permute-start | bytes 24584 | tf_op jit(solution)/shard_map/ppermute | solution.py:33
  47.9 4.0 %collective-permute-start.8 = (f16[8,512]{1,0:T(8,128)(2,1)S(1)}, f16[8,512]{1,0:T(8,128)(2,1)S(1)}, u32[]{:S(2)}, u32[]{:S(2)}) collective-permute-start(f16[8,512]{1,0:T(8,128)(2,1)S(1)} %get-tuple-element.31), channel_id=1, source_target_pairs={{0,32},{16,48},{32,0},{48,16},{1,33},{17,49},{33,1},{49,17},{2,34}... | collective-permute-start | bytes 24584 | tf_op jit(solution)/shard_map/ppermute | solution.py:33
  48.4 3.7 %collective-permute-start.9 = (f16[8,512]{1,0:T(8,128)(2,1)S(1)}, f16[8,512]{1,0:T(8,128)(2,1)S(1)}, u32[]{:S(2)}, u32[]{:S(2)}) collective-permute-start(f16[8,512]{1,0:T(8,128)(2,1)S(1)} %get-tuple-element.33), channel_id=1, source_target_pairs={{0,16},{16,32},{32,48},{48,0},{1,17},{17,33},{33,49},{49,1},{2,18}... | collective-permute-start | bytes 24584 | tf_op jit(solution)/shard_map/ppermute | solution.py:33
  62.9 20.8 %all-to-all-start.2 = ((f32[256,1,9]{2,1,0:T(1,128)}), f32[256,1,9]{2,1,0:T(1,128)S(1)}, u32[]{:S(2)}, u32[]{:S(2)}) async-start(f32[256,1,9]{2,1,0:T(1,128)} %broadcast_in_dim.4), calls=%async_computation.2 | async-start | bytes 262144 | tf_op jit(solution)/shard_map/all_to_all | solution.py:37
  85.4 19.2 %all-to-all-start.3 = ((bf16[8,8,3328]{2,1,0:T(8,128)(2,1)}), bf16[8,8,3328]{2,1,0:T(8,128)(2,1)S(1)}, u32[]{:S(2)}, u32[]{:S(2)}) async-start(bf16[8,8,3328]{2,1,0:T(8,128)(2,1)} %get-tuple-element.19), calls=%async_computation.3 | async-start | bytes 851968 | tf_op jit(solution)/shard_map/all_to_all | solution.py:37
  88.8 4.1 %collective-permute-start.15 = (bf16[8,768]{1,0:T(8,128)(2,1)S(1)}, bf16[8,768]{1,0:T(8,128)(2,1)S(1)}, u32[]{:S(2)}, u32[]{:S(2)}) collective-permute-start(bf16[8,768]{1,0:T(8,128)(2,1)S(1)} %get-tuple-element.20), channel_id=1, source_target_pairs={{0,32},{16,48},{32,0},{48,16},{1,33},{17,49},{33,1},{49,17},{2,34}... | collective-permute-start | bytes 36872 | tf_op jit(solution)/shard_map/ppermute | solution.py:33
  89.5 3.8 %collective-permute-start.16 = (bf16[8,768]{1,0:T(8,128)(2,1)S(1)}, bf16[8,768]{1,0:T(8,128)(2,1)S(1)}, u32[]{:S(2)}, u32[]{:S(2)}) collective-permute-start(bf16[8,768]{1,0:T(8,128)(2,1)S(1)} %get-tuple-element.20), channel_id=1, source_target_pairs={{0,16},{16,32},{32,48},{48,0},{1,17},{17,33},{33,49},{49,1},{2,18}... | collective-permute-start | bytes 36872 | tf_op jit(solution)/shard_map/ppermute | solution.py:33
  90.0 3.3 %collective-permute-start.17 = (bf16[8,768]{1,0:T(8,128)(2,1)S(1)}, bf16[8,768]{1,0:T(8,128)(2,1)S(1)}, u32[]{:S(2)}, u32[]{:S(2)}) collective-permute-start(bf16[8,768]{1,0:T(8,128)(2,1)S(1)} %get-tuple-element.20), channel_id=1, source_target_pairs={{0,48},{16,0},{32,16},{48,32},{1,49},{17,1},{33,17},{49,33},{2,50}... | collective-permute-start | bytes 36872 | tf_op jit(solution)/shard_map/ppermute | solution.py:33
  105.3 18.5 %all-to-all-start.4 = ((bf16[8,4,8,768]{3,2,1,0:T(8,128)(2,1)}), bf16[8,4,8,768]{3,2,1,0:T(8,128)(2,1)S(1)}, u32[]{:S(2)}, u32[]{:S(2)}) async-start(bf16[8,4,8,768]{3,2,1,0:T(8,128)(2,1)} %broadcast_in_dim.5), calls=%async_computation.4 | async-start | bytes 786432 | tf_op jit(solution)/shard_map/all_to_all | solution.py:37
  108.8 15.6 %collective-permute-start.20 = (bf16[8,8,3328]{2,1,0:T(8,128)(2,1)S(1)}, bf16[8,8,3328]{2,1,0:T(8,128)(2,1)S(1)}, u32[]{:S(2)}, u32[]{:S(2)}) collective-permute-start(bf16[8,8,3328]{2,1,0:T(8,128)(2,1)S(1)} %all-to-all-done.3.refs_1_), channel_id=1, source_target_pairs={{0,32},{16,48},{32,0},{48,16},{1,33},{17,49},{33,1},{49,17},{2,34}... | collective-permute-start | bytes 1277960 | tf_op jit(solution)/shard_map/ppermute | solution.py:33
  109.5 21.7 %collective-permute-start.11 = (bf16[8,8,3328]{2,1,0:T(8,128)(2,1)S(1)}, bf16[8,8,3328]{2,1,0:T(8,128)(2,1)S(1)}, u32[]{:S(2)}, u32[]{:S(2)}) collective-permute-start(bf16[8,8,3328]{2,1,0:T(8,128)(2,1)S(1)} %all-to-all-done.3.refs_1_), channel_id=1, source_target_pairs={{0,16},{16,32},{32,48},{48,0},{1,17},{17,33},{33,49},{49,1},{2,18}... | collective-permute-start | bytes 1277960 | tf_op jit(solution)/shard_map/ppermute | solution.py:33
  109.5 22.2 %collective-permute-start.13 = (bf16[8,8,3328]{2,1,0:T(8,128)(2,1)S(1)}, bf16[8,8,3328]{2,1,0:T(8,128)(2,1)S(1)}, u32[]{:S(2)}, u32[]{:S(2)}) collective-permute-start(bf16[8,8,3328]{2,1,0:T(8,128)(2,1)S(1)} %all-to-all-done.3.refs_1_), channel_id=1, source_target_pairs={{0,48},{16,0},{32,16},{48,32},{1,49},{17,1},{33,17},{49,33},{2,50}... | collective-permute-start | bytes 1277960 | tf_op jit(solution)/shard_map/ppermute | solution.py:33
  123.8 12.7 %collective-permute-start.18 = (bf16[8,4,8,768]{3,2,1,0:T(8,128)(2,1)S(1)}, bf16[8,4,8,768]{3,2,1,0:T(8,128)(2,1)S(1)}, u32[]{:S(2)}, u32[]{:S(2)}) collective-permute-start(bf16[8,4,8,768]{3,2,1,0:T(8,128)(2,1)S(1)} %all-to-all-done.4.refs_3_), channel_id=1, source_target_pairs={{0,1},{1,0},{2,3},{3,2},{4,5},{5,4},{6,7},{7,6},{8,9},{9,8},{10,11... | collective-permute-start | bytes 1179656 | tf_op jit(solution)/shard_map/ppermute | solution.py:28
  124.3 8.8 %collective-permute-start.19 = (bf16[8,8,3328]{2,1,0:T(8,128)(2,1)S(1)}, bf16[8,8,3328]{2,1,0:T(8,128)(2,1)S(1)}, u32[]{:S(2)}, u32[]{:S(2)}) collective-permute-start(bf16[8,8,3328]{2,1,0:T(8,128)(2,1)S(1)} %all-to-all-done.3.refs_1_), channel_id=1, source_target_pairs={{0,1},{1,0},{2,3},{3,2},{4,5},{5,4},{6,7},{7,6},{8,9},{9,8},{10,11... | collective-permute-start | bytes 1277960 | tf_op jit(solution)/shard_map/ppermute | solution.py:28
  124.3 8.8 %collective-permute-start.21 = (bf16[8,8,3328]{2,1,0:T(8,128)(2,1)S(1)}, bf16[8,8,3328]{2,1,0:T(8,128)(2,1)S(1)}, u32[]{:S(2)}, u32[]{:S(2)}) collective-permute-start(bf16[8,8,3328]{2,1,0:T(8,128)(2,1)S(1)} %collective-permute-done.20.refs_3_), channel_id=1, source_target_pairs={{0,1},{1,0},{2,3},{3,2},{4,5},{5,4},{6,7},{7,6},{8,9},{9,8},{10,11... | collective-permute-start | bytes 1277960 | tf_op jit(solution)/shard_map/ppermute | solution.py:28
  131.2 5.3 %collective-permute-start.12 = (bf16[8,8,3328]{2,1,0:T(8,128)(2,1)S(1)}, bf16[8,8,3328]{2,1,0:T(8,128)(2,1)S(1)}, u32[]{:S(2)}, u32[]{:S(2)}) collective-permute-start(bf16[8,8,3328]{2,1,0:T(8,128)(2,1)S(1)} %collective-permute-done.11.refs_1_), channel_id=1, source_target_pairs={{0,1},{1,0},{2,3},{3,2},{4,5},{5,4},{6,7},{7,6},{8,9},{9,8},{10,11... | collective-permute-start | bytes 1277960 | tf_op jit(solution)/shard_map/ppermute | solution.py:28
  131.7 4.8 %collective-permute-start.14 = (bf16[8,8,3328]{2,1,0:T(8,128)(2,1)S(1)}, bf16[8,8,3328]{2,1,0:T(8,128)(2,1)S(1)}, u32[]{:S(2)}, u32[]{:S(2)}) collective-permute-start(bf16[8,8,3328]{2,1,0:T(8,128)(2,1)S(1)} %collective-permute-done.13.refs_2_), channel_id=1, source_target_pairs={{0,1},{1,0},{2,3},{3,2},{4,5},{5,4},{6,7},{7,6},{8,9},{9,8},{10,11... | collective-permute-start | bytes 1277960 | tf_op jit(solution)/shard_map/ppermute | solution.py:28
  (7 other events, 273.4 us)
